TPU v7x, 32 devices: a whole 2x2x4 slice. The times are simulated.
32 devices in a mesh: leaf: 8 (over z, y), hand: 4 (over x, core).
Axes of the slice: x: 2, y: 2, z: 4, core: 2. Of those that a mesh axis runs over, the one named last changes fastest.
Arguments:
- opp_range: float32 [1024], P('hand'), may hold values from 0.1 to 1
- br_range: float32 [1024], P('hand'), may hold values from 0.001 to 1
- up_weight: bfloat16 [4, 256, 1024], P(None, 'leaf', 'hand'), may hold values from 0.29882812 to 1
- up_parent: int32 [3, 256], replicated, may hold values from 0 to 255
- board_cards: int32 [768, 5], P('leaf'), may hold values from 0 to 51, as said below
- hand_rank: int32 [768, 1024], P('leaf'), may hold values from 0 to 7461
- root_parent: int32 [768], P('leaf'), may hold values from 0 to 255
- br_actions: int32 [768], P('leaf'), may hold values from 1 to 8
- opp_actions: int32 [768, 8], P('leaf'), may hold values from 1 to 8
- leaf_kind: int32 [768, 8, 8], P('leaf'), may hold values from 0 to 1
- leaf_stake: int32 [768, 8, 8], P('leaf'), may hold values from 1 to 400
- opp_weight: bfloat16 [768, 8, 8, 1024], P('leaf', None, None, 'hand'), may hold values from 0.049804688 to 1
Outputs:
- level_values: float32 [4, 256, 1024], P(None, 'leaf', 'hand')
- root_value: float32 [1024], P('hand')
- best_value: float32 [], replicated
Inputs may be any that keep to these rules, and one draw needn't show every extreme that they name: `board_cards`: five different cards for each subtree.
All inputs are finite; a program needn't handle non-finite values.
Results may differ from a plain program's by a relative error of at most 0.0003.
Values may be sent and summed in bfloat16 or wider, within the bound.
A program may use at most 128 MiB of HBM per device.

v0:
```python
import functools

import jax
import jax.numpy as jnp
import numpy as np
from jax import lax
from jax.experimental import pallas as pl
from jax.experimental.pallas import tpu as pltpu
from jax.sharding import PartitionSpec as P

PAYOFF_UNIT = 1.0 / 4096.0
VMEM_LIMIT = 60 * 1024 * 1024
F32 = jnp.float32
BF16 = jnp.bfloat16


def hand_cards(number):
    low_list = []
    high_list = []
    for low_card in range(52):
        for high_card in range(low_card + 1, 52):
            low_list.append(low_card)
            high_list.append(high_card)
    chosen = np.arange(number) * 1326 // number
    cards = np.zeros((8, number), np.float32)
    cards[0] = np.array(low_list)[chosen]
    cards[1] = np.array(high_list)[chosen]
    cards[2] = np.exp2(np.arange(number) * 0.6180339887498949 % 1.0)
    cards[3] = 1.0 / cards[2]
    return cards


def vmem():
    return pl.BlockSpec(memory_space=pltpu.VMEM)


def hbm():
    return pl.BlockSpec(memory_space=pl.ANY)


def greet(axes_sizes):
    barrier = pltpu.get_barrier_semaphore()
    count = 0
    for axis, size in axes_sizes:
        me = lax.axis_index(axis)
        for dist in range(1, size):
            pl.semaphore_signal(
                barrier,
                inc=1,
                device_id={axis: lax.rem(me + dist, size)},
                device_id_type=pl.DeviceIdType.MESH,
            )
            count += 1
    pl.semaphore_wait(barrier, count)


def push(axis, size, source, target, sem):
    me = lax.axis_index(axis)
    copies = []
    for dist in range(1, size):
        peer = lax.rem(me + dist, size)
        copies.append(push_one(axis, peer, source(peer), target, sem, dist))
    return copies


def push_one(axis, peer, source, target, sem, dist):
    send_sem, recv_sem = sem
    copy = pltpu.make_async_remote_copy(
        src_ref=source,
        dst_ref=target,
        send_sem=send_sem.at[dist - 1],
        recv_sem=recv_sem.at[dist - 1],
        device_id={axis: peer},
        device_id_type=pl.DeviceIdType.MESH,
    )
    copy.start()
    return copy


def sems(*shape):
    return pltpu.SemaphoreType.DMA(shape[:-1] + (max(shape[-1] - 1, 1),))


def columns_of(ref, pad_ref):
    lines, count = ref.shape
    pad_ref[...] = jnp.zeros(pad_ref.shape, F32)
    pad_ref[0:lines, 0:count] = ref[...].astype(F32)
    return pad_ref[...].T


def opponent_kernel(
    leafs, hands, levels, actions,
    upper_ref, parent_ref, root_ref, board_ref, range_ref, cards_ref, opp_ref, kind_ref, stake_ref, weight_ref,
    ratio_out, reach_out, anc_out,
    every, weights, ratio, reach, anc, pad, stake_lines, stake_rows,
    up_s, up_r, anc_s, anc_r, ratio_s, ratio_r, reach_s, reach_r, load_sem, own_sem,
):
    leaf = lax.axis_index("leaf")
    hand = lax.axis_index("hand")
    mine = weights.shape[1]
    width = weights.shape[3]
    boards = hands * mine
    span = actions * actions
    both = 2 * actions
    nodes_dev = upper_ref.shape[1]
    nodes = leafs * nodes_dev

    loads = []
    for dist in range(hands):
        part = lax.rem(hand + dist + 1, hands)
        load = pltpu.make_async_copy(
            weight_ref.at[pl.ds(part * mine, mine)], weights.at[part], load_sem.at[dist]
        )
        load.start()
        loads.append(load)
    own_upper = pltpu.make_async_copy(upper_ref, every.at[leaf], own_sem.at[0])
    own_upper.start()
    greet((("leaf", leafs), ("hand", hands)))
    up_copies = push("leaf", leafs, lambda peer: upper_ref, every.at[leaf], (up_s, up_r))

    stake_lines[...] = jnp.zeros(stake_lines.shape, F32)
    reply_ids = lax.broadcasted_iota(jnp.int32, (actions, boards), 0)
    for a in range(actions):
        lines = slice(a * actions, (a + 1) * actions)
        stake = stake_ref[lines, :]
        signed = jnp.where(kind_ref[lines, :] == 1, stake, -stake)
        legal = reply_ids < opp_ref[a : a + 1, :]
        stake_lines[lines, 0:boards] = jnp.where(legal, signed, 0).astype(F32)
    stake_rows[...] = stake_lines[...].T

    node_column = lax.broadcasted_iota(jnp.int32, (nodes, boards), 0)
    anc[...] = jnp.zeros(anc.shape, F32)
    line = root_ref[...]
    anc[levels - 1 : levels, 0:boards] = line.astype(F32)
    for level in range(levels - 2, -1, -1):
        parents = jnp.broadcast_to(parent_ref[level : level + 1, :], (8, nodes)).astype(F32)
        column = parents.T[:, 0:1]
        line_f = jnp.sum(jnp.where(node_column == line, column, 0.0), axis=0, keepdims=True)
        anc[level : level + 1, 0:boards] = line_f
        line = line_f.astype(jnp.int32)
    anc_columns = anc[...].T.astype(jnp.int32)

    diagonal = lax.broadcasted_iota(jnp.int32, (actions, span), 0) == (
        lax.broadcasted_iota(jnp.int32, (actions, span), 1) // actions
    )

    own_lanes = pl.ds(pl.multiple_of(hand * width, width), width)
    spread = cards_ref[2:3, own_lanes]

    def fold_part(part, target):
        def eight(k, carry):
            lines = stake_rows[pl.ds(pl.multiple_of(part * mine + k * 8, 8), 8), :]
            for i in range(8):
                stake = jnp.broadcast_to(lines[i : i + 1, :], (actions, span))
                stake = jnp.where(diagonal, stake, 0.0)
                legal = jnp.where(stake != 0.0, 1.0, 0.0)
                shown = jnp.maximum(stake, 0.0)
                fold = jnp.maximum(-stake, 0.0)
                shown_hi = jnp.floor(shown * 0.5) * 2.0
                fold_hi = jnp.floor(fold * 0.5) * 2.0
                rows = jnp.concatenate([legal, shown_hi, shown - shown_hi, fold_hi, fold - fold_hi], axis=0)
                sums = jnp.dot(rows.astype(BF16), weights[part, k * 8 + i], preferred_element_type=F32)
                piece = [sums[j * actions : (j + 1) * actions] for j in range(5)]
                scale = spread / piece[0]
                pair = jnp.concatenate(
                    [(piece[1] + piece[2]) * scale, (piece[3] + piece[4]) * scale], axis=0
                )
                place = pl.multiple_of((k * 8 + i) * both, both)
                target[part, pl.ds(place, both), :] = pair.astype(BF16)
            return carry

        lax.fori_loop(0, mine // 8, eight, 0)

    ratio_copies = []
    for dist in range(1, hands):
        part = lax.rem(hand + dist, hands)
        loads[dist - 1].wait()
        fold_part(part, ratio)
        ratio_copies.append(
            push_one("hand", part, ratio.at[part], ratio_out.at[hand], (ratio_s, ratio_r), dist)
        )
    anc_copies = push("leaf", leafs, lambda peer: anc, anc_out.at[leaf], (anc_s, anc_r))
    anc_out[leaf] = anc[...]

    low = cards_ref[0:1, own_lanes]
    high = cards_ref[1:2, own_lanes]
    board_columns = columns_of(board_ref, pad)
    free = jnp.ones((boards, width), F32)
    for card in range(5):
        column = board_columns[0:boards, card : card + 1]
        free = jnp.where((column == low) | (column == high), 0.0, free)

    own_upper.wait()
    for copy in up_copies:
        copy.wait()
    node_ids = lax.broadcasted_iota(jnp.int32, (boards, nodes), 1)
    total = jnp.broadcast_to(range_ref[...], (boards, width))
    for level in range(levels):
        pick = jnp.where(anc_columns[0:boards, level : level + 1] == node_ids, 1.0, 0.0).astype(BF16)
        table = every[:, level].reshape(nodes, width)
        total = total * jnp.dot(pick, table, preferred_element_type=F32)
    total = total * (free * cards_ref[3:4, own_lanes])
    for part in range(hands):
        reach[part] = total[part * mine : (part + 1) * mine]
    reach_copies = push("hand", hands, lambda peer: reach.at[peer], reach_out.at[hand], (reach_s, reach_r))
    reach_out[hand] = reach[hand]

    loads[hands - 1].wait()
    fold_part(hand, ratio)
    ratio_out[hand] = ratio[hand]
    for copy in anc_copies + ratio_copies + reach_copies:
        copy.wait()


def opponent(upper, parents, roots, boards, opp_range, cards, opp_actions, kinds, stakes, weights, leafs, hands, actions):
    levels, nodes_dev, width = upper.shape
    count, span, _ = weights.shape
    mine = count // hands
    lanes = -(-count // 128) * 128
    return pl.pallas_call(
        functools.partial(opponent_kernel, leafs, hands, levels, actions),
        out_shape=(
            jax.ShapeDtypeStruct((hands, mine * 2 * actions, width), BF16),
            jax.ShapeDtypeStruct((hands, mine, width), F32),
            jax.ShapeDtypeStruct((leafs, 8, lanes), F32),
        ),
        in_specs=[vmem()] * 9 + [hbm()],
        out_specs=(vmem(), vmem(), vmem()),
        scratch_shapes=[
            pltpu.VMEM((leafs, levels, nodes_dev, width), BF16),
            pltpu.VMEM((hands, mine, span, width), BF16),
            pltpu.VMEM((hands, mine * 2 * actions, width), BF16),
            pltpu.VMEM((hands, mine, width), F32),
            pltpu.VMEM((8, lanes), F32),
            pltpu.VMEM((8, lanes), F32),
            pltpu.VMEM((span, lanes), F32),
            pltpu.VMEM((lanes, span), F32),
            sems(leafs), sems(leafs), sems(leafs), sems(leafs),
            sems(hands), sems(hands), sems(hands), sems(hands),
            pltpu.SemaphoreType.DMA((hands,)),
            pltpu.SemaphoreType.DMA((1,)),
        ],
        compiler_params=pltpu.CompilerParams(
            collective_id=0, has_side_effects=True, vmem_limit_bytes=VMEM_LIMIT
        ),
        name="opponent",
    )(upper, parents, roots, boards, opp_range, cards, opp_actions, kinds, stakes, weights)


def responder_kernel(
    hands, leafs, levels, nodes_dev, actions,
    ratio_ref, reach_ref, anc_ref, actions_ref, rank_ref, board_ref, cards_ref, range_ref,
    level_out, root_out, best_out,
    apart_ref, pad, board_columns, ready, mine, every, tally,
    hand_s, hand_r, leaf_s, leaf_r, best_s, best_r, own_sem,
):
    hand = lax.axis_index("hand")
    leaf = lax.axis_index("leaf")
    _, count, width = mine.shape
    all_hands = rank_ref.shape[1]
    both = 2 * actions
    chunks = count // 8
    low = cards_ref[0:1, :]
    high = cards_ref[1:2, :]
    columns = cards_ref[...].T
    for part in range(hands):
        rows = slice(part * width, (part + 1) * width)
        low_col = columns[rows, 0:1]
        high_col = columns[rows, 1:2]
        hit = (low_col == low) | (low_col == high) | (high_col == low) | (high_col == high)
        apart_ref[rows, :] = jnp.where(hit, 0.0, 1.0).astype(BF16)
    board_columns[...] = columns_of(board_ref, pad)
    greet((("hand", hands), ("leaf", leafs)))
    action_ids = lax.broadcasted_iota(jnp.int32, (actions, 1), 0)

    def values(chunk, midway):
        first = pl.multiple_of(hand * count + chunk * 8, 8)
        cards_on = board_columns[pl.ds(first, 8), :]
        free = jnp.ones((8, all_hands), F32)
        for card in range(5):
            column = cards_on[:, card : card + 1]
            free = jnp.where((column == low) | (column == high), 0.0, free)
        ranks = rank_ref[pl.ds(first, 8), :].astype(F32)
        rank_columns = ranks.T
        lines = []
        folded = jnp.zeros((8 * both, all_hands), F32)
        for part in range(hands):
            pieces = []
            for i in range(8):
                b = chunk * 8 + i
                row = ratio_ref[part, b * both : (b + 1) * both, :].astype(F32)
                pieces.append((row * reach_ref[part, b : b + 1, :]).astype(BF16))
            lines.append(pieces)
            folded = folded + jnp.dot(
                jnp.concatenate(pieces, axis=0),
                apart_ref[part * width : (part + 1) * width, :],
                preferred_element_type=F32,
            )
        best_rows = []
        for i in range(8):
            if i == 4:
                midway()
            shown = jnp.zeros((both, all_hands), F32)
            for part in range(hands):
                rows = slice(part * width, (part + 1) * width)
                apart = apart_ref[rows, :]
                order = (ranks[i : i + 1, :] - rank_columns[rows, i : i + 1]).astype(BF16)
                order = jnp.minimum(jnp.maximum(order, -apart), apart)
                shown = shown + jnp.dot(lines[part][i], order, preferred_element_type=F32)
            per_node = shown[0:actions] + folded[i * both + actions : (i + 1) * both]
            allowed = action_ids < actions_ref[first + i]
            best_rows.append(jnp.max(jnp.where(allowed, per_node, -1e30), axis=0, keepdims=True))
        best = jnp.concatenate(best_rows, axis=0) * (free * PAYOFF_UNIT)
        for part in range(hands):
            ready[part, chunk * 8 : (chunk + 1) * 8, :] = best[:, part * width : (part + 1) * width]

    def to_hands(chunk):
        rows = pl.ds(chunk * 8, 8)
        copies = push(
            "hand", hands, lambda peer: ready.at[peer, rows], mine.at[hand, rows],
            (hand_s.at[chunk], hand_r.at[chunk]),
        )
        mine[hand, chunk * 8 : (chunk + 1) * 8, :] = ready[hand, chunk * 8 : (chunk + 1) * 8, :]
        return copies

    def to_leafs(chunk, copies):
        for copy in copies:
            copy.wait()
        rows = pl.ds(chunk * 8, 8)
        return push(
            "leaf", leafs, lambda peer: mine.at[:, rows], every.at[leaf, :, rows],
            (leaf_s.at[chunk], leaf_r.at[chunk]),
        )

    leaf_copies = []
    hand_copies = []

    def relay(chunk):
        if chunk >= 0:
            leaf_copies.extend(to_leafs(chunk, hand_copies))

    for chunk in range(chunks):
        values(chunk, functools.partial(relay, chunk - 1))
        hand_copies = to_hands(chunk)
    leaf_copies += to_leafs(chunks - 1, hand_copies)
    every[leaf] = mine[...]

    boards = hands * count
    node_ids = leaf * nodes_dev + lax.broadcasted_iota(jnp.int32, (nodes_dev, boards), 0)
    node_ids = node_ids.astype(F32)
    for copy in leaf_copies:
        copy.wait()

    def add_leaf(source, carry):
        sums, total = carry
        block = every[source].reshape(boards, width)
        coarse = block.astype(BF16)
        fine = (block - coarse.astype(F32)).astype(BF16)
        lines = anc_ref[source]
        pick = jnp.concatenate(
            [jnp.where(lines[k : k + 1, 0:boards] == node_ids, 1.0, 0.0) for k in range(levels)], axis=0
        ).astype(BF16)
        sums = sums + jnp.dot(pick, coarse, preferred_element_type=F32)
        sums = sums + jnp.dot(pick, fine, preferred_element_type=F32)
        return sums, total + jnp.sum(block, axis=0, keepdims=True)

    start = (jnp.zeros((levels * nodes_dev, width), F32), jnp.zeros((1, width), F32))
    sums, total = lax.fori_loop(0, leafs, add_leaf, start)
    root = total / (nodes_dev * leafs)
    root_out[...] = root
    weight = range_ref[...]
    tally[hand] = jnp.concatenate(
        [
            jnp.broadcast_to(jnp.sum(weight * root, axis=1, keepdims=True), (8, 128)),
            jnp.broadcast_to(jnp.sum(weight, axis=1, keepdims=True), (8, 128)),
        ],
        axis=0,
    )
    copies = push("hand", hands, lambda peer: tally.at[hand], tally.at[hand], (best_s, best_r))
    for k in range(levels):
        level_out[k] = sums[k * nodes_dev : (k + 1) * nodes_dev]
    for copy in copies:
        copy.wait()
    pair = jnp.sum(tally[...], axis=0)
    best_out[...] = pair[0:1, 0:1] / pair[8:9, 0:1]


def responder(ratio, reach, ancestors, br_actions, ranks, boards, cards, br_range, leafs, hands, nodes_dev, levels, actions):
    _, count, width = reach.shape
    all_hands = ranks.shape[1]
    lanes = ancestors.shape[2]
    chunks = count // 8
    return pl.pallas_call(
        functools.partial(responder_kernel, hands, leafs, levels, nodes_dev, actions),
        out_shape=(
            jax.ShapeDtypeStruct((levels, nodes_dev, width), F32),
            jax.ShapeDtypeStruct((1, width), F32),
            jax.ShapeDtypeStruct((1, 1), F32),
        ),
        in_specs=[vmem()] * 3 + [pl.BlockSpec(memory_space=pltpu.SMEM)] + [vmem()] * 4,
        out_specs=(vmem(), vmem(), vmem()),
        scratch_shapes=[
            pltpu.VMEM((all_hands, all_hands), BF16),
            pltpu.VMEM((8, lanes), F32),
            pltpu.VMEM((lanes, 8), F32),
            pltpu.VMEM((hands, count, width), F32),
            pltpu.VMEM((hands, count, width), F32),
            pltpu.VMEM((leafs, hands, count, width), F32),
            pltpu.VMEM((hands, 16, 128), F32),
            sems(chunks, hands), sems(chunks, hands), sems(chunks, leafs), sems(chunks, leafs),
            sems(hands), sems(hands),
            pltpu.SemaphoreType.DMA(()),
        ],
        compiler_params=pltpu.CompilerParams(
            collective_id=1, has_side_effects=True, vmem_limit_bytes=VMEM_LIMIT
        ),
        name="responder",
    )(ratio, reach, ancestors, br_actions, ranks, boards, cards, br_range)


def local(
    opp_range,
    br_range,
    up_weight,
    up_parent,
    board_cards,
    hand_rank,
    root_parent,
    br_actions,
    opp_actions,
    leaf_kind,
    leaf_stake,
    opp_weight,
):
    levels, nodes_dev, hands_dev = up_weight.shape
    boards_dev, hands_all = hand_rank.shape
    actions = opp_actions.shape[1]
    span = actions * actions
    leafs = lax.axis_size("leaf")
    hands = lax.axis_size("hand")
    cards = jnp.asarray(hand_cards(hands_all))
    boards = board_cards.T
    ratio, reach, ancestors = opponent(
        up_weight,
        up_parent,
        root_parent[None, :],
        boards,
        opp_range[None, :],
        cards,
        opp_actions.T,
        leaf_kind.transpose(1, 2, 0).reshape(span, boards_dev),
        leaf_stake.transpose(1, 2, 0).reshape(span, boards_dev),
        opp_weight.reshape(boards_dev, span, hands_dev),
        leafs,
        hands,
        actions,
    )
    level_values, root, best = responder(
        ratio,
        reach,
        ancestors,
        br_actions,
        hand_rank,
        boards,
        cards,
        br_range[None, :],
        leafs,
        hands,
        nodes_dev,
        levels,
        actions,
    )
    return (level_values, root[0], best[0, 0])


def solution(mesh):
    in_specs = (
        P("hand"),
        P("hand"),
        P(None, "leaf", "hand"),
        P(),
        P("leaf", None),
        P("leaf", None),
        P("leaf"),
        P("leaf"),
        P("leaf", None),
        P("leaf", None, None),
        P("leaf", None, None),
        P("leaf", None, None, "hand"),
    )
    out_specs = (P(None, "leaf", "hand"), P("hand"), P())
    return jax.shard_map(local, mesh=mesh, in_specs=in_specs, out_specs=out_specs, check_vma=False)
```

profile of v0, /device:TPU:0, one launch (start us, length us, event | category | flops | bytes accessed | tf_op | source)
XLA Modules:
  0.0 65.9 jit_solution(14380121518327457121)
XLA Ops:
  0.6 21.8 %opponent.1 = (bf16[4,384,256]{2,1,0:T(8,128)(2,1)}, f32[4,24,256]{2,1,0:T(8,128)}, f32[8,8,128]{2,1,0:T(8,128)}) custom-call(bf16[4,32,256]{2,1,0:T(8,128)(2,1)} %upper_ref.1, s32[3,256]{1,0:T(4,128)} %parent_ref.1, s32[1,96]{1,0:T(1,128)} %bitcast.23, s32[5,96]{1,0:T(8,128)} %bitcast.17, f32[1,256]{1,0:T(1,128)} %bitcast.20, ...), custom_call_target="tpu_custom_call" | custom-call | tf_op jit(solution)/shard_map/opponent/pallas_call | solution.py:220
  22.4 38.9 %responder.1 = (f32[4,32,256]{2,1,0:T(8,128)}, f32[1,256]{1,0:T(1,128)}, f32[1,1]{1,0:T(1,128)}) custom-call(bf16[4,384,256]{2,1,0:T(8,128)(2,1)} %get-tuple-element.9.ratio_ref, f32[4,24,256]{2,1,0:T(8,128)} %get-tuple-element.10.reach_ref, f32[8,8,128]{2,1,0:T(8,128)} %get-tuple-element.11.anc_ref, s32[96]{0:T(128)} %actions_ref.1, s32[96,1024]{1,0:T(8,128)} %rank_ref.1, ...), custom_call_target="tpu_custom_call" | custom-call | tf_op jit(solution)/shard_map/responder/pallas_call | solution.py:393
  61.4 1.6 %copy.19 = f32[4,32,256]{2,1,0:T(8,128)} copy(f32[4,32,256]{2,1,0:T(8,128)} %get-tuple-element.18) | data formatting | bytes 262144
  62.9 1.2 %copy.20 = f32[256]{0:T(256)} copy(f32[256]{0:T(256)} %bitcast.21) | data formatting | bytes 2048
where the time goes:
time: 66.1 us; the launch traced here: 65.9 us
  Pallas kernels  60.7 us (92%)
  local copies, waits for them, and re-layouts  2.78 us (4%)
  between operations  2.41 us (4%)
    pallas_call x1, Pallas kernels, responder(): pl.pallas_call(functools.partial(responder_kernel, hands, leafs, levels,...  38.9 us
    pallas_call x1, Pallas kernels, opponent(): pl.pallas_call(functools.partial(opponent_kernel, leafs, hands, levels, a...  21.8 us
    unnamed x2, local copies, waits for them, and re-layouts  2.78 us

commit v1 on v0

v1 whole, which is shorter than its diff:
```python
import functools

import jax
import jax.numpy as jnp
import numpy as np
from jax import lax
from jax.experimental import pallas as pl
from jax.experimental.pallas import tpu as pltpu
from jax.sharding import PartitionSpec as P

PAYOFF_UNIT = 1.0 / 4096.0
VMEM_LIMIT = 60 * 1024 * 1024
F32 = jnp.float32
BF16 = jnp.bfloat16


def hand_cards(number):
    low_list = []
    high_list = []
    for low_card in range(52):
        for high_card in range(low_card + 1, 52):
            low_list.append(low_card)
            high_list.append(high_card)
    chosen = np.arange(number) * 1326 // number
    cards = np.zeros((8, number), np.float32)
    cards[0] = np.array(low_list)[chosen]
    cards[1] = np.array(high_list)[chosen]
    cards[2] = np.exp2(np.arange(number) * 0.6180339887498949 % 1.0)
    cards[3] = 1.0 / cards[2]
    return cards


def vmem():
    return pl.BlockSpec(memory_space=pltpu.VMEM)


def hbm():
    return pl.BlockSpec(memory_space=pl.ANY)


def greet(axes_sizes):
    barrier = pltpu.get_barrier_semaphore()
    count = 0
    for axis, size in axes_sizes:
        me = lax.axis_index(axis)
        for dist in range(1, size):
            pl.semaphore_signal(
                barrier,
                inc=1,
                device_id={axis: lax.rem(me + dist, size)},
                device_id_type=pl.DeviceIdType.MESH,
            )
            count += 1
    pl.semaphore_wait(barrier, count)


def flip(index, mask):
    out = index
    bit = 1
    while bit <= mask:
        if mask & bit:
            out = out + bit - 2 * bit * lax.rem(index // bit, 2)
        bit *= 2
    return out


def peers_of(me, size):
    if size & (size - 1):
        return [lax.rem(me + dist, size) for dist in range(1, size)]
    far = [mask for mask in range(1, size) if mask >= size // 2]
    near = [mask for mask in range(1, size) if mask < size // 2]
    return [flip(me, mask) for mask in far + near]


def push(axis, size, source, target, sem):
    me = lax.axis_index(axis)
    copies = []
    for k in range(size - 1):
        peer = lax.rem(me + k + 1, size)
        copies.append(push_one(axis, peer, source(peer), target, sem, k))
    return copies


def push_one(axis, peer, source, target, sem, k):
    send_sem, recv_sem = sem
    copy = pltpu.make_async_remote_copy(
        src_ref=source,
        dst_ref=target,
        send_sem=send_sem.at[k],
        recv_sem=recv_sem.at[k],
        device_id={axis: peer},
        device_id_type=pl.DeviceIdType.MESH,
    )
    copy.start()
    return copy


def sems(*shape):
    return pltpu.SemaphoreType.DMA(shape[:-1] + (max(shape[-1] - 1, 1),))


def columns_of(ref, pad_ref):
    lines, count = ref.shape
    pad_ref[...] = jnp.zeros(pad_ref.shape, F32)
    pad_ref[0:lines, 0:count] = ref[...].astype(F32)
    return pad_ref[...].T


def kernel(
    leafs, hands, levels, actions,
    upper_ref, parent_ref, root_ref, board_ref, range_ref, br_ref, cards_ref, opp_ref, kind_ref, stake_ref,
    actions_ref, rank_ref, weight_ref,
    level_out, root_out, best_out,
    every, weights, ranks_in, ratio, ratio_in, reach, reach_in, anc, anc_all, br_all,
    pad, board_columns, stake_lines, stake_rows, apart_ref, against_ref, scaled,
    ready, mine, values_all, tally, tally_leaf, tally_all,
    up_s, up_r, anc_s, anc_r, ratio_s, ratio_r, reach_s, reach_r, br_s, br_r,
    hand_s, hand_r, leaf_s, leaf_r, tally_s, tally_r, total_s, total_r, load_sem, own_sem,
):
    leaf = lax.axis_index("leaf")
    hand = lax.axis_index("hand")
    count = ratio.shape[1] // (2 * actions)
    width = weights.shape[3]
    boards = hands * count
    chunks = count // 8
    all_hands = hands * width
    span = actions * actions
    both = 2 * actions
    nodes_dev = upper_ref.shape[1]
    nodes = leafs * nodes_dev
    partners = peers_of(hand, hands)

    def load(part, chunk, slot):
        first = pl.multiple_of(part * count + chunk * 8, 8)
        return pltpu.make_async_copy(
            weight_ref.at[pl.ds(first, 8)], weights.at[part, pl.ds(chunk * 8, 8)], load_sem.at[slot, chunk]
        )

    parts = partners + [hand]
    for chunk in range(chunks):
        for k, part in enumerate(parts):
            load(part, chunk, k).start()
    own_upper = pltpu.make_async_copy(upper_ref, every.at[leaf], own_sem.at[0])
    own_upper.start()
    own_ranks = pltpu.make_async_copy(
        rank_ref.at[pl.ds(pl.multiple_of(hand * count, 8), count)], ranks_in, own_sem.at[1]
    )
    own_ranks.start()
    greet((("leaf", leafs), ("hand", hands)))
    up_copies = push("leaf", leafs, lambda peer: upper_ref, every.at[leaf], (up_s, up_r))

    stake_lines[...] = jnp.zeros(stake_lines.shape, F32)
    reply_ids = lax.broadcasted_iota(jnp.int32, (actions, boards), 0)
    for a in range(actions):
        lines = slice(a * actions, (a + 1) * actions)
        stake = stake_ref[lines, :]
        signed = jnp.where(kind_ref[lines, :] == 1, stake, -stake)
        legal = reply_ids < opp_ref[a : a + 1, :]
        stake_lines[lines, 0:boards] = jnp.where(legal, signed, 0).astype(F32)
    stake_rows[...] = stake_lines[...].T

    diagonal = lax.broadcasted_iota(jnp.int32, (actions, span), 0) == (
        lax.broadcasted_iota(jnp.int32, (actions, span), 1) // actions
    )
    own_lanes = pl.ds(pl.multiple_of(hand * width, width), width)
    spread = cards_ref[2:3, own_lanes]

    def fold(part, chunk, target):
        lines = stake_rows[pl.ds(pl.multiple_of(part * count + chunk * 8, 8), 8), :]
        for i in range(8):
            stake = jnp.broadcast_to(lines[i : i + 1, :], (actions, span))
            stake = jnp.where(diagonal, stake, 0.0)
            legal = jnp.where(stake != 0.0, 1.0, 0.0)
            shown = jnp.maximum(stake, 0.0)
            folds = jnp.maximum(-stake, 0.0)
            shown_hi = jnp.floor(shown * 0.5) * 2.0
            fold_hi = jnp.floor(folds * 0.5) * 2.0
            rows = jnp.concatenate([legal, shown_hi, shown - shown_hi, fold_hi, folds - fold_hi], axis=0)
            sums = jnp.dot(rows.astype(BF16), weights[part, chunk * 8 + i], preferred_element_type=F32)
            piece = [sums[j * actions : (j + 1) * actions] for j in range(5)]
            scale = spread / piece[0]
            pair = jnp.concatenate(
                [(piece[1] + piece[2]) * scale, (piece[3] + piece[4]) * scale], axis=0
            )
            place = (chunk * 8 + i) * both
            target[part, place : place + both, :] = pair.astype(BF16)

    ratio_copies = []
    for chunk in range(chunks):
        block = pl.ds(chunk * 8 * both, 8 * both)
        for k, part in enumerate(partners):
            load(part, chunk, k).wait()
            fold(part, chunk, ratio)
            ratio_copies.append(
                push_one(
                    "hand", part, ratio.at[part, block], ratio_in.at[hand, block],
                    (ratio_s.at[chunk], ratio_r.at[chunk]), k,
                )
            )
    br_copies = push("hand", hands, lambda peer: br_ref, br_all.at[hand], (br_s, br_r))
    br_all[hand] = br_ref[...]

    node_column = lax.broadcasted_iota(jnp.int32, (nodes, boards), 0)
    pad[...] = jnp.zeros(pad.shape, F32)
    line = root_ref[...]
    pad[levels - 1 : levels, 0:boards] = line.astype(F32)
    for level in range(levels - 2, -1, -1):
        parents = jnp.broadcast_to(parent_ref[level : level + 1, :], (8, nodes)).astype(F32)
        column = parents.T[:, 0:1]
        line_f = jnp.sum(jnp.where(node_column == line, column, 0.0), axis=0, keepdims=True)
        pad[level : level + 1, 0:boards] = line_f
        line = line_f.astype(jnp.int32)
    anc_float = pad[...].T
    anc_columns = anc_float.astype(jnp.int32)
    lane = lax.broadcasted_iota(jnp.int32, (boards, boards), 1)
    held = (lane % (hands * 8)) // 8 * count + lane // (hands * 8) * 8 + lane % 8
    moved = lax.broadcasted_iota(jnp.int32, (boards, boards), 0) == held
    anc[...] = jnp.zeros(anc.shape, F32)
    for level in range(levels):
        anc[level : level + 1, 0:boards] = jnp.sum(
            jnp.where(moved, anc_float[0:boards, level : level + 1], 0.0), axis=0, keepdims=True
        )
    anc_copies = push("leaf", leafs, lambda peer: anc, anc_all.at[leaf], (anc_s, anc_r))
    anc_all[leaf] = anc[...]

    low = cards_ref[0:1, :]
    high = cards_ref[1:2, :]
    card_columns = cards_ref[...].T
    for part in range(hands):
        rows = slice(part * width, (part + 1) * width)
        low_col = card_columns[rows, 0:1]
        high_col = card_columns[rows, 1:2]
        hit = (low_col == low) | (low_col == high) | (high_col == low) | (high_col == high)
        apart_ref[rows, :] = jnp.where(hit, 0.0, 1.0).astype(BF16)
        against_ref[rows, :] = jnp.where(hit, 0.0, -1.0).astype(BF16)

    for chunk in range(chunks):
        load(hand, chunk, hands - 1).wait()
        fold(hand, chunk, ratio_in)

    own_low = cards_ref[0:1, own_lanes]
    own_high = cards_ref[1:2, own_lanes]
    board_columns[...] = columns_of(board_ref, pad)
    free = jnp.ones((boards, width), F32)
    for card in range(5):
        column = board_columns[0:boards, card : card + 1]
        free = jnp.where((column == own_low) | (column == own_high), 0.0, free)
    free = free * cards_ref[3:4, own_lanes]

    own_ranks.wait()
    ranks = ((ranks_in[...] % 128) + 128).astype(F32)
    octave = ranks_in[...] // 128
    for bit in (1, 2, 4, 8, 16, 32):
        ranks = ranks * jnp.where(octave // bit % 2 == 1, float(2**bit), 1.0)
    scaled[...] = ranks

    own_upper.wait()
    for copy in up_copies:
        copy.wait()
    node_ids = lax.broadcasted_iota(jnp.int32, (boards, nodes), 1)
    total = jnp.broadcast_to(range_ref[...], (boards, width))
    for level in range(levels):
        pick = jnp.where(anc_columns[0:boards, level : level + 1] == node_ids, 1.0, 0.0).astype(BF16)
        table = every[:, level].reshape(nodes, width)
        total = total * jnp.dot(pick, table, preferred_element_type=F32)
    total = total * free
    for part in range(hands):
        reach[part] = total[part * count : (part + 1) * count].astype(BF16)
    reach_copies = []
    for k, part in enumerate(partners):
        reach_copies.append(
            push_one("hand", part, reach.at[part], reach_in.at[hand], (reach_s, reach_r), k)
        )
    reach_in[hand] = reach[hand]
    action_ids = lax.broadcasted_iota(jnp.int32, (actions, 1), 0)
    for copy in br_copies:
        copy.wait()
    br_row = jnp.concatenate([br_all[part] for part in range(hands)], axis=1)
    for copy in reach_copies:
        copy.wait()

    def values(chunk, midway):
        first = pl.multiple_of(hand * count + chunk * 8, 8)
        cards_on = board_columns[pl.ds(first, 8), :]
        open_hands = jnp.ones((8, all_hands), F32)
        for card in range(5):
            column = cards_on[:, card : card + 1]
            open_hands = jnp.where((column == low) | (column == high), 0.0, open_hands)
        rank_rows = scaled[chunk * 8 : chunk * 8 + 8, :]
        rank_columns = rank_rows.T.astype(BF16)
        rank_rows = rank_rows.astype(BF16)
        lines = []
        folded = jnp.zeros((8 * both, all_hands), F32)
        for part in range(hands):
            pieces = []
            reach_rows = reach_in[part, chunk * 8 : chunk * 8 + 8, :].astype(F32)
            for i in range(8):
                b = chunk * 8 + i
                row = ratio_in[part, b * both : (b + 1) * both, :].astype(F32)
                pieces.append((row * reach_rows[i : i + 1, :]).astype(BF16))
            lines.append(pieces)
            folded = folded + jnp.dot(
                jnp.concatenate(pieces, axis=0),
                apart_ref[part * width : (part + 1) * width, :],
                preferred_element_type=F32,
            )
        best_rows = []
        for i in range(8):
            if i == 4:
                midway()
            shown = jnp.zeros((both, all_hands), F32)
            for part in range(hands):
                rows = slice(part * width, (part + 1) * width)
                order = rank_rows[i : i + 1, :] - rank_columns[rows, i : i + 1]
                order = jnp.minimum(jnp.maximum(order, against_ref[rows, :]), apart_ref[rows, :])
                shown = shown + jnp.dot(lines[part][i], order, preferred_element_type=F32)
            per_node = shown[0:actions] + folded[i * both + actions : (i + 1) * both]
            allowed = action_ids < actions_ref[first + i]
            best_rows.append(jnp.max(jnp.where(allowed, per_node, -1e30), axis=0, keepdims=True))
        best = jnp.concatenate(best_rows, axis=0) * (open_hands * PAYOFF_UNIT)
        for part in range(hands):
            ready[chunk, part] = best[:, part * width : (part + 1) * width]
        return jnp.sum(best * br_row, axis=1, keepdims=True)

    def to_hands(chunk):
        copies = [
            push_one(
                "hand", part, ready.at[chunk, part], mine.at[chunk, hand],
                (hand_s.at[chunk], hand_r.at[chunk]), k,
            )
            for k, part in enumerate(partners)
        ]
        mine[chunk, hand] = ready[chunk, hand]
        return copies

    def to_leafs(chunk, copies):
        for copy in copies:
            copy.wait()
        copies = push(
            "leaf", leafs, lambda peer: mine.at[chunk], values_all.at[chunk, leaf],
            (leaf_s.at[chunk], leaf_r.at[chunk]),
        )
        values_all[chunk, leaf] = mine[chunk]
        return copies

    leaf_copies = []
    hand_copies = []

    def relay(chunk):
        if chunk >= 0:
            leaf_copies.append(to_leafs(chunk, hand_copies))

    weighed = jnp.zeros((8, 1), F32)
    for chunk in range(chunks):
        for copy in ratio_copies[chunk * (hands - 1) : (chunk + 1) * (hands - 1)]:
            copy.wait()
        weighed = weighed + values(chunk, functools.partial(relay, chunk - 1))
        if chunk == chunks - 1:
            share = jnp.broadcast_to(jnp.sum(weighed, axis=0, keepdims=True), (1, 128))
            tally[hand, 0:1] = share
            tally_copies = [
                push_one(
                    "hand", part, tally.at[hand, pl.ds(0, 1)], tally.at[hand, pl.ds(0, 1)], (tally_s, tally_r), k
                )
                for k, part in enumerate(partners)
            ]
        hand_copies = to_hands(chunk)
    leaf_copies.append(to_leafs(chunks - 1, hand_copies))
    for copy in tally_copies:
        copy.wait()
    tally_leaf[0:1, :] = sum(tally[part, 0:1] for part in range(hands))
    total_copies = push(
        "leaf", leafs, lambda peer: tally_leaf.at[pl.ds(0, 1)], tally_all.at[leaf, pl.ds(0, 1)], (total_s, total_r)
    )
    tally_all[leaf, 0:1] = tally_leaf[0:1, :]

    for copy in anc_copies:
        copy.wait()
    lines_dev = levels * nodes_dev
    block = hands * 8
    node_rows = leaf * nodes_dev + lax.broadcasted_iota(jnp.int32, (nodes_dev, block), 0)
    node_rows = node_rows.astype(F32)

    def add_chunk(chunk, sums):
        def add_leaf(source, sums):
            part = values_all[chunk, source].reshape(block, width)
            coarse = part.astype(BF16)
            fine = (part - coarse.astype(F32)).astype(BF16)
            lines = anc_all[source][:, chunk * block : (chunk + 1) * block]
            pick = [jnp.where(lines[k : k + 1, :] == node_rows, 1.0, 0.0) for k in range(levels)]
            pick = jnp.concatenate(pick + [jnp.ones((8, block), F32)], axis=0).astype(BF16)
            sums = sums + jnp.dot(pick, coarse, preferred_element_type=F32)
            return sums + jnp.dot(pick, fine, preferred_element_type=F32)

        for source in range(leafs):
            sums = add_leaf(source, sums)
        return sums

    sums = jnp.zeros((lines_dev + 8, width), F32)
    for chunk in range(chunks):
        for copy in leaf_copies[chunk]:
            copy.wait()
        sums = add_chunk(chunk, sums)
    root_out[...] = sums[lines_dev : lines_dev + 1] / nodes
    for k in range(levels):
        level_out[k] = sums[k * nodes_dev : (k + 1) * nodes_dev]
    for copy in total_copies:
        copy.wait()
    whole = sum(tally_all[source, 0:1] for source in range(leafs)) / nodes
    best_out[...] = whole[:, 0:1] / jnp.sum(br_row, axis=1, keepdims=True)


def evaluate(
    upper, parents, roots, boards, opp_range, br_range, cards, opp_actions, kinds, stakes,
    br_actions, ranks, weights, leafs, hands, actions,
):
    levels, nodes_dev, width = upper.shape
    boards_dev, span, _ = weights.shape
    count = boards_dev // hands
    chunks = count // 8
    both = 2 * actions
    all_hands = ranks.shape[1]
    lanes = -(-boards_dev // 128) * 128
    return pl.pallas_call(
        functools.partial(kernel, leafs, hands, levels, actions),
        out_shape=(
            jax.ShapeDtypeStruct((levels, nodes_dev, width), F32),
            jax.ShapeDtypeStruct((1, width), F32),
            jax.ShapeDtypeStruct((1, 1), F32),
        ),
        in_specs=[vmem()] * 10 + [pl.BlockSpec(memory_space=pltpu.SMEM), hbm(), hbm()],
        out_specs=(vmem(), vmem(), vmem()),
        scratch_shapes=[
            pltpu.VMEM((leafs, levels, nodes_dev, width), BF16),
            pltpu.VMEM((hands, count, span, width), BF16),
            pltpu.VMEM((count, all_hands), jnp.int32),
            pltpu.VMEM((hands, count * both, width), BF16),
            pltpu.VMEM((hands, count * both, width), BF16),
            pltpu.VMEM((hands, count, width), BF16),
            pltpu.VMEM((hands, count, width), BF16),
            pltpu.VMEM((8, lanes), F32),
            pltpu.VMEM((leafs, 8, lanes), F32),
            pltpu.VMEM((hands, 1, width), F32),
            pltpu.VMEM((8, lanes), F32),
            pltpu.VMEM((lanes, 8), F32),
            pltpu.VMEM((span, lanes), F32),
            pltpu.VMEM((lanes, span), F32),
            pltpu.VMEM((all_hands, all_hands), BF16),
            pltpu.VMEM((all_hands, all_hands), BF16),
            pltpu.VMEM((count, all_hands), F32),
            pltpu.VMEM((chunks, hands, 8, width), F32),
            pltpu.VMEM((chunks, hands, 8, width), F32),
            pltpu.VMEM((chunks, leafs, hands, 8, width), F32),
            pltpu.VMEM((hands, 8, 128), F32),
            pltpu.VMEM((8, 128), F32),
            pltpu.VMEM((leafs, 8, 128), F32),
            sems(leafs), sems(leafs), sems(leafs), sems(leafs),
            sems(chunks, hands), sems(chunks, hands), sems(hands), sems(hands), sems(hands), sems(hands),
            sems(chunks, hands), sems(chunks, hands), sems(chunks, leafs), sems(chunks, leafs),
            sems(hands), sems(hands), sems(leafs), sems(leafs),
            pltpu.SemaphoreType.DMA((hands, chunks)),
            pltpu.SemaphoreType.DMA((2,)),
        ],
        compiler_params=pltpu.CompilerParams(
            collective_id=0, has_side_effects=True, vmem_limit_bytes=VMEM_LIMIT
        ),
        name="evaluate",
    )(
        upper, parents, roots, boards, opp_range, br_range, cards, opp_actions, kinds, stakes,
        br_actions, ranks, weights,
    )


def local(
    opp_range,
    br_range,
    up_weight,
    up_parent,
    board_cards,
    hand_rank,
    root_parent,
    br_actions,
    opp_actions,
    leaf_kind,
    leaf_stake,
    opp_weight,
):
    hands_dev = up_weight.shape[2]
    boards_dev, hands_all = hand_rank.shape
    actions = opp_actions.shape[1]
    span = actions * actions
    leafs = lax.axis_size("leaf")
    hands = lax.axis_size("hand")
    cards = jnp.asarray(hand_cards(hands_all))
    boards = board_cards.T
    level_values, root, best = evaluate(
        up_weight,
        up_parent,
        root_parent[None, :],
        boards,
        opp_range[None, :],
        br_range[None, :],
        cards,
        opp_actions.T,
        leaf_kind.transpose(1, 2, 0).reshape(span, boards_dev),
        leaf_stake.transpose(1, 2, 0).reshape(span, boards_dev),
        br_actions,
        hand_rank,
        opp_weight.reshape(boards_dev, span, hands_dev),
        leafs,
        hands,
        actions,
    )
    return (level_values, root[0], best[0, 0])


def solution(mesh):
    in_specs = (
        P("hand"),
        P("hand"),
        P(None, "leaf", "hand"),
        P(),
        P("leaf", None),
        P("leaf", None),
        P("leaf"),
        P("leaf"),
        P("leaf", None),
        P("leaf", None, None),
        P("leaf", None, None),
        P("leaf", None, None, "hand"),
    )
    out_specs = (P(None, "leaf", "hand"), P("hand"), P())
    return jax.shard_map(local, mesh=mesh, in_specs=in_specs, out_specs=out_specs, check_vma=False)
```

time: 66.1 us -> 55.3 us (0.84)
  Pallas kernels: 60.7 us -> 49.9 us
    pallas_call x2 -> x1, Pallas kernels: 60.7 us -> 49.9 us  [evaluate(): pl.pallas_call(functools.partial(kernel, leafs, hands, levels, actions),...]
where the time goes in v1:
time: 55.3 us; the launch traced here: 55.1 us
  Pallas kernels  49.9 us (90%)
  local copies, waits for them, and re-layouts  2.8 us (5%)
  between operations  2.4 us (4%)
    pallas_call x1, Pallas kernels, evaluate(): pl.pallas_call(functools.partial(kernel, leafs, hands, levels, actions),...  49.9 us
    unnamed x2, local copies, waits for them, and re-layouts  2.8 us

profile of v1, /device:TPU:0, one launch (start us, length us, event | category | flops | bytes accessed | tf_op | source)
XLA Modules:
  0.0 55.1 jit_solution(17201302133807031754)
XLA Ops:
  0.6 49.9 %evaluate.1 = (f32[4,32,256]{2,1,0:T(8,128)}, f32[1,256]{1,0:T(1,128)}, f32[1,1]{1,0:T(1,128)}) custom-call(bf16[4,32,256]{2,1,0:T(8,128)(2,1)} %upper_ref.1, s32[3,256]{1,0:T(4,128)} %parent_ref.1, s32[1,96]{1,0:T(1,128)} %bitcast.22, s32[5,96]{1,0:T(8,128)} %bitcast.17, f32[1,256]{1,0:T(1,128)} %bitcast.19, f32[1,256]{1,0:T(1,128)} %bitcast.20, ...), custom_call_target="tpu_custom_call" | custom-call | tf_op jit(solution)/shard_map/evaluate/pallas_call | solution.py:424
  50.5 1.6 %copy.19 = f32[4,32,256]{2,1,0:T(8,128)} copy(f32[4,32,256]{2,1,0:T(8,128)} %get-tuple-element.12) | data formatting | bytes 262144
  52.1 1.2 %copy.20 = f32[256]{0:T(256)} copy(f32[256]{0:T(256)} %bitcast.21) | data formatting | bytes 2048

commit v2 on v1

--- a/solution.py
+++ b/solution.py
@@ -72,31 +72,25 @@
     return [flip(me, mask) for mask in far + near]
 
 
-def push(axis, size, source, target, sem):
-    me = lax.axis_index(axis)
-    copies = []
-    for k in range(size - 1):
-        peer = lax.rem(me + k + 1, size)
-        copies.append(push_one(axis, peer, source(peer), target, sem, k))
-    return copies
-
-
-def push_one(axis, peer, source, target, sem, k):
+def push(axis, peers, source, target, sem):
+    for peer in peers:
+        send(axis, peer, source(peer), target, sem).start()
+
+
+def send(axis, peer, source, target, sem):
     send_sem, recv_sem = sem
-    copy = pltpu.make_async_remote_copy(
+    return pltpu.make_async_remote_copy(
         src_ref=source,
         dst_ref=target,
-        send_sem=send_sem.at[k],
-        recv_sem=recv_sem.at[k],
+        send_sem=send_sem,
+        recv_sem=recv_sem,
         device_id={axis: peer},
         device_id_type=pl.DeviceIdType.MESH,
     )
-    copy.start()
-    return copy
-
-
-def sems(*shape):
-    return pltpu.SemaphoreType.DMA(shape[:-1] + (max(shape[-1] - 1, 1),))
+
+
+def settle(ref, sem):
+    pltpu.make_async_copy(ref, ref, sem).wait()
 
 
 def columns_of(ref, pad_ref):
@@ -113,9 +107,9 @@
     level_out, root_out, best_out,
     every, weights, ranks_in, ratio, ratio_in, reach, reach_in, anc, anc_all, br_all,
     pad, board_columns, stake_lines, stake_rows, apart_ref, against_ref, scaled,
-    ready, mine, values_all, tally, tally_leaf, tally_all,
-    up_s, up_r, anc_s, anc_r, ratio_s, ratio_r, reach_s, reach_r, br_s, br_r,
-    hand_s, hand_r, leaf_s, leaf_r, tally_s, tally_r, total_s, total_r, load_sem, own_sem,
+    ready, values_all, units, units_all,
+    up_s, up_r, pass_r, anc_s, anc_r, ratio_s, ratio_r, reach_s, reach_r, br_s, br_r,
+    value_s, value_r, unit_s, unit_r, load_sem, own_sem,
 ):
     leaf = lax.axis_index("leaf")
     hand = lax.axis_index("hand")
@@ -129,17 +123,18 @@
     nodes_dev = upper_ref.shape[1]
     nodes = leafs * nodes_dev
     partners = peers_of(hand, hands)
-
-    def load(part, chunk, slot):
+    others = [lax.rem(leaf + dist, leafs) for dist in range(1, leafs)]
+
+    def load(part, chunk):
         first = pl.multiple_of(part * count + chunk * 8, 8)
         return pltpu.make_async_copy(
-            weight_ref.at[pl.ds(first, 8)], weights.at[part, pl.ds(chunk * 8, 8)], load_sem.at[slot, chunk]
+            weight_ref.at[pl.ds(first, 8)], weights.at[part, pl.ds(chunk * 8, 8)], load_sem.at[chunk]
         )
 
     parts = partners + [hand]
     for chunk in range(chunks):
-        for k, part in enumerate(parts):
-            load(part, chunk, k).start()
+        for part in parts:
+            load(part, chunk).start()
     own_upper = pltpu.make_async_copy(upper_ref, every.at[leaf], own_sem.at[0])
     own_upper.start()
     own_ranks = pltpu.make_async_copy(
@@ -147,7 +142,34 @@
     )
     own_ranks.start()
     greet((("leaf", leafs), ("hand", hands)))
-    up_copies = push("leaf", leafs, lambda peer: upper_ref, every.at[leaf], (up_s, up_r))
+    ring = leafs // 2
+    side = lax.rem(leaf, 2)
+    twin = leaf + 1 - 2 * side
+
+    def up_copy(source, owner, peer, k):
+        return pltpu.make_async_remote_copy(
+            src_ref=source,
+            dst_ref=every.at[owner],
+            send_sem=up_s,
+            recv_sem=pass_r if k is None else up_r.at[k],
+            device_id={"leaf": peer},
+            device_id_type=pl.DeviceIdType.MESH,
+        )
+
+    def around(dist):
+        return lax.rem(leaf // 2 + dist, ring) * 2 + side
+
+    steps = sorted(range(1, ring), key=lambda dist: min(dist, ring - dist))
+    up_direct = {dist: up_copy(upper_ref, leaf, around(dist), dist) for dist in steps}
+    up_direct[0] = up_copy(upper_ref, leaf, twin, 0)
+    for dist in steps + [0]:
+        up_direct[dist].start()
+
+    def pass_on(dists):
+        for dist in dists:
+            up_direct[dist].wait_recv()
+            origin = around(ring - dist)
+            up_copy(every.at[origin], origin, twin, None).start()
 
     stake_lines[...] = jnp.zeros(stake_lines.shape, F32)
     reply_ids = lax.broadcasted_iota(jnp.int32, (actions, boards), 0)
@@ -185,19 +207,15 @@
             place = (chunk * 8 + i) * both
             target[part, place : place + both, :] = pair.astype(BF16)
 
-    ratio_copies = []
     for chunk in range(chunks):
         block = pl.ds(chunk * 8 * both, 8 * both)
-        for k, part in enumerate(partners):
-            load(part, chunk, k).wait()
+        settle(weights.at[:, pl.ds(chunk * 8, 8)], load_sem.at[chunk])
+        for part in partners:
             fold(part, chunk, ratio)
-            ratio_copies.append(
-                push_one(
-                    "hand", part, ratio.at[part, block], ratio_in.at[hand, block],
-                    (ratio_s.at[chunk], ratio_r.at[chunk]), k,
-                )
-            )
-    br_copies = push("hand", hands, lambda peer: br_ref, br_all.at[hand], (br_s, br_r))
+            send(
+                "hand", part, ratio.at[part, block], ratio_in.at[hand, block], (ratio_s, ratio_r.at[chunk])
+            ).start()
+    push("hand", partners, lambda peer: br_ref, br_all.at[hand], (br_s, br_r))
     br_all[hand] = br_ref[...]
 
     node_column = lax.broadcasted_iota(jnp.int32, (nodes, boards), 0)
@@ -220,13 +238,15 @@
         anc[level : level + 1, 0:boards] = jnp.sum(
             jnp.where(moved, anc_float[0:boards, level : level + 1], 0.0), axis=0, keepdims=True
         )
-    anc_copies = push("leaf", leafs, lambda peer: anc, anc_all.at[leaf], (anc_s, anc_r))
+    push("leaf", others, lambda peer: anc, anc_all.at[leaf], (anc_s, anc_r))
     anc_all[leaf] = anc[...]
 
     low = cards_ref[0:1, :]
     high = cards_ref[1:2, :]
     card_columns = cards_ref[...].T
     for part in range(hands):
+        if part == hands // 2:
+            pass_on([dist for dist in steps if dist in (1, ring - 1)])
         rows = slice(part * width, (part + 1) * width)
         low_col = card_columns[rows, 0:1]
         high_col = card_columns[rows, 1:2]
@@ -234,8 +254,8 @@
         apart_ref[rows, :] = jnp.where(hit, 0.0, 1.0).astype(BF16)
         against_ref[rows, :] = jnp.where(hit, 0.0, -1.0).astype(BF16)
 
+    pass_on([dist for dist in steps if dist not in (1, ring - 1)])
     for chunk in range(chunks):
-        load(hand, chunk, hands - 1).wait()
         fold(hand, chunk, ratio_in)
 
     own_low = cards_ref[0:1, own_lanes]
@@ -255,8 +275,9 @@
     scaled[...] = ranks
 
     own_upper.wait()
-    for copy in up_copies:
-        copy.wait()
+    up_direct[0].wait_recv()
+    settle(every.at[pl.ds(0, ring - 1)], pass_r)
+    settle(every.at[pl.ds(0, leafs - 1)], up_s)
     node_ids = lax.broadcasted_iota(jnp.int32, (boards, nodes), 1)
     total = jnp.broadcast_to(range_ref[...], (boards, width))
     for level in range(levels):
@@ -265,38 +286,34 @@
         total = total * jnp.dot(pick, table, preferred_element_type=F32)
     total = total * free
     for part in range(hands):
-        reach[part] = total[part * count : (part + 1) * count].astype(BF16)
-    reach_copies = []
-    for k, part in enumerate(partners):
-        reach_copies.append(
-            push_one("hand", part, reach.at[part], reach_in.at[hand], (reach_s, reach_r), k)
-        )
+        for chunk in range(chunks):
+            first = part * count + chunk * 8
+            reach[part, chunk] = total[first : first + 8].astype(BF16)
+    push("hand", partners, lambda peer: reach.at[peer], reach_in.at[hand], (reach_s, reach_r))
     reach_in[hand] = reach[hand]
     action_ids = lax.broadcasted_iota(jnp.int32, (actions, 1), 0)
-    for copy in br_copies:
-        copy.wait()
+    settle(br_all.at[pl.ds(0, hands - 1)], br_r)
     br_row = jnp.concatenate([br_all[part] for part in range(hands)], axis=1)
-    for copy in reach_copies:
-        copy.wait()
-
-    def values(chunk, midway):
+    settle(reach.at[pl.ds(0, hands - 1)], reach_r)
+
+    def values(chunk):
         first = pl.multiple_of(hand * count + chunk * 8, 8)
         cards_on = board_columns[pl.ds(first, 8), :]
         open_hands = jnp.ones((8, all_hands), F32)
         for card in range(5):
             column = cards_on[:, card : card + 1]
             open_hands = jnp.where((column == low) | (column == high), 0.0, open_hands)
-        rank_rows = scaled[chunk * 8 : chunk * 8 + 8, :]
+        rank_rows = scaled[pl.ds(pl.multiple_of(chunk * 8, 8), 8), :]
         rank_columns = rank_rows.T.astype(BF16)
         rank_rows = rank_rows.astype(BF16)
         lines = []
         folded = jnp.zeros((8 * both, all_hands), F32)
         for part in range(hands):
             pieces = []
-            reach_rows = reach_in[part, chunk * 8 : chunk * 8 + 8, :].astype(F32)
+            reach_rows = reach_in[part, chunk].astype(F32)
             for i in range(8):
                 b = chunk * 8 + i
-                row = ratio_in[part, b * both : (b + 1) * both, :].astype(F32)
+                row = ratio_in[part, pl.ds(pl.multiple_of(b * both, both), both), :].astype(F32)
                 pieces.append((row * reach_rows[i : i + 1, :]).astype(BF16))
             lines.append(pieces)
             folded = folded + jnp.dot(
@@ -306,8 +323,6 @@
             )
         best_rows = []
         for i in range(8):
-            if i == 4:
-                midway()
             shown = jnp.zeros((both, all_hands), F32)
             for part in range(hands):
                 rows = slice(part * width, (part + 1) * width)
@@ -318,96 +333,97 @@
             allowed = action_ids < actions_ref[first + i]
             best_rows.append(jnp.max(jnp.where(allowed, per_node, -1e30), axis=0, keepdims=True))
         best = jnp.concatenate(best_rows, axis=0) * (open_hands * PAYOFF_UNIT)
+        peak = jnp.max(jnp.abs(best), axis=1, keepdims=True) * (1.0 / 32640.0)
+        unit = jnp.full((8, 1), 2.0**16, F32)
+        inverse = jnp.full((8, 1), 2.0**-16, F32)
+        for bit in (64, 32, 16, 8, 4, 2, 1):
+            fits = peak <= unit * 2.0**-bit
+            unit = jnp.where(fits, unit * 2.0**-bit, unit)
+            inverse = jnp.where(fits, inverse * 2.0**bit, inverse)
+        codes = jnp.floor(best * inverse + 0.5).astype(jnp.int32).astype(jnp.int16)
         for part in range(hands):
-            ready[chunk, part] = best[:, part * width : (part + 1) * width]
-        return jnp.sum(best * br_row, axis=1, keepdims=True)
-
-    def to_hands(chunk):
-        copies = [
-            push_one(
-                "hand", part, ready.at[chunk, part], mine.at[chunk, hand],
-                (hand_s.at[chunk], hand_r.at[chunk]), k,
-            )
-            for k, part in enumerate(partners)
-        ]
-        mine[chunk, hand] = ready[chunk, hand]
-        return copies
-
-    def to_leafs(chunk, copies):
-        for copy in copies:
-            copy.wait()
-        copies = push(
-            "leaf", leafs, lambda peer: mine.at[chunk], values_all.at[chunk, leaf],
-            (leaf_s.at[chunk], leaf_r.at[chunk]),
-        )
-        values_all[chunk, leaf] = mine[chunk]
-        return copies
-
-    leaf_copies = []
-    hand_copies = []
-
-    def relay(chunk):
-        if chunk >= 0:
-            leaf_copies.append(to_leafs(chunk, hand_copies))
-
-    weighed = jnp.zeros((8, 1), F32)
-    for chunk in range(chunks):
-        for copy in ratio_copies[chunk * (hands - 1) : (chunk + 1) * (hands - 1)]:
-            copy.wait()
-        weighed = weighed + values(chunk, functools.partial(relay, chunk - 1))
-        if chunk == chunks - 1:
-            share = jnp.broadcast_to(jnp.sum(weighed, axis=0, keepdims=True), (1, 128))
-            tally[hand, 0:1] = share
-            tally_copies = [
-                push_one(
-                    "hand", part, tally.at[hand, pl.ds(0, 1)], tally.at[hand, pl.ds(0, 1)], (tally_s, tally_r), k
-                )
-                for k, part in enumerate(partners)
-            ]
-        hand_copies = to_hands(chunk)
-    leaf_copies.append(to_leafs(chunks - 1, hand_copies))
-    for copy in tally_copies:
-        copy.wait()
-    tally_leaf[0:1, :] = sum(tally[part, 0:1] for part in range(hands))
-    total_copies = push(
-        "leaf", leafs, lambda peer: tally_leaf.at[pl.ds(0, 1)], tally_all.at[leaf, pl.ds(0, 1)], (total_s, total_r)
-    )
-    tally_all[leaf, 0:1] = tally_leaf[0:1, :]
-
-    for copy in anc_copies:
-        copy.wait()
+            ready[chunk, part] = codes[:, part * width : (part + 1) * width]
+        share = jnp.sum(jnp.sum(best * br_row, axis=1, keepdims=True), axis=0, keepdims=True)
+        lane = lax.broadcasted_iota(jnp.int32, (8, 128), 1)
+        place = hand * 8 + lax.broadcasted_iota(jnp.int32, (8, 128), 0)
+        row = jnp.sum(jnp.where(lane == place, unit, 0.0), axis=0, keepdims=True)
+        units[chunk] = jnp.where(lane[0:1] == hands * 8, share, row)
+
+    peers = leafs * hands
+
+    def send_values(chunk, k):
+        to_hand = lax.rem(hand + k % hands, hands)
+        target = {"leaf": lax.rem(leaf + k // hands, leafs), "hand": to_hand}
+        pltpu.make_async_remote_copy(
+            src_ref=ready.at[chunk, to_hand],
+            dst_ref=values_all.at[chunk, leaf * hands + hand],
+            send_sem=value_s,
+            recv_sem=value_r.at[chunk],
+            device_id=target,
+            device_id_type=pl.DeviceIdType.MESH,
+        ).start()
+        pltpu.make_async_remote_copy(
+            src_ref=units.at[chunk],
+            dst_ref=units_all.at[chunk, leaf * hands + hand],
+            send_sem=unit_s,
+            recv_sem=unit_r.at[chunk],
+            device_id=target,
+            device_id_type=pl.DeviceIdType.MESH,
+        ).start()
+
+    def one_chunk(chunk, carry):
+        settle(ratio.at[pl.ds(0, hands - 1), pl.ds(0, 8 * both)], ratio_r.at[chunk])
+        values(chunk)
+
+        def one(k, carry):
+            send_values(chunk, k)
+            return carry
+
+        lax.fori_loop(1, peers, one, 0, unroll=peers <= 32)
+        values_all[chunk, leaf * hands + hand] = ready[chunk, hand]
+        units_all[chunk, leaf * hands + hand] = units[chunk]
+        return carry
+
+    lax.fori_loop(0, chunks, one_chunk, 0)
+    settle(ratio.at[pl.ds(0, hands - 1)], ratio_s)
+    settle(reach.at[pl.ds(0, hands - 1)], reach_s)
+    settle(br_all.at[pl.ds(0, hands - 1)], br_s)
+
+    settle(anc_all.at[pl.ds(0, leafs - 1)], anc_r)
+    settle(anc_all.at[pl.ds(0, leafs - 1)], anc_s)
     lines_dev = levels * nodes_dev
     block = hands * 8
     node_rows = leaf * nodes_dev + lax.broadcasted_iota(jnp.int32, (nodes_dev, block), 0)
     node_rows = node_rows.astype(F32)
 
-    def add_chunk(chunk, sums):
-        def add_leaf(source, sums):
-            part = values_all[chunk, source].reshape(block, width)
-            coarse = part.astype(BF16)
-            fine = (part - coarse.astype(F32)).astype(BF16)
-            lines = anc_all[source][:, chunk * block : (chunk + 1) * block]
-            pick = [jnp.where(lines[k : k + 1, :] == node_rows, 1.0, 0.0) for k in range(levels)]
-            pick = jnp.concatenate(pick + [jnp.ones((8, block), F32)], axis=0).astype(BF16)
-            sums = sums + jnp.dot(pick, coarse, preferred_element_type=F32)
-            return sums + jnp.dot(pick, fine, preferred_element_type=F32)
-
+    def add_leaf(chunk, source, sums):
+        own = pl.ds(source * hands, hands)
+        part = values_all[chunk, own].astype(jnp.int32).astype(F32).reshape(block, width)
+        coarse = part.astype(BF16)
+        fine = (part - coarse.astype(F32)).astype(BF16)
+        lines = anc_all[source][:, chunk * block : (chunk + 1) * block]
+        row = jnp.sum(units_all[chunk, own], axis=0)
+        unit = row[:, 0:block]
+        pick = [jnp.where(lines[k : k + 1, :] == node_rows, unit, 0.0) for k in range(levels)]
+        pick = jnp.concatenate(pick + [jnp.broadcast_to(unit, (8, block))], axis=0).astype(BF16)
+        sums = sums + jnp.dot(pick, coarse, preferred_element_type=F32)
+        return sums + jnp.dot(pick, fine, preferred_element_type=F32), row[:, block : block + 1]
+
+    sums = jnp.zeros((lines_dev + 8, width), F32)
+    whole = jnp.zeros((1, 1), F32)
+    for chunk in range(chunks):
+        settle(values_all.at[chunk, pl.ds(0, peers - 1)], value_r.at[chunk])
+        settle(units_all.at[chunk, pl.ds(0, peers - 1)], unit_r.at[chunk])
         for source in range(leafs):
-            sums = add_leaf(source, sums)
-        return sums
-
-    sums = jnp.zeros((lines_dev + 8, width), F32)
-    for chunk in range(chunks):
-        for copy in leaf_copies[chunk]:
-            copy.wait()
-        sums = add_chunk(chunk, sums)
+            sums, share = add_leaf(chunk, source, sums)
+            whole = whole + share
     root_out[...] = sums[lines_dev : lines_dev + 1] / nodes
     for k in range(levels):
         level_out[k] = sums[k * nodes_dev : (k + 1) * nodes_dev]
-    for copy in total_copies:
-        copy.wait()
-    whole = sum(tally_all[source, 0:1] for source in range(leafs)) / nodes
-    best_out[...] = whole[:, 0:1] / jnp.sum(br_row, axis=1, keepdims=True)
+    for chunk in range(chunks):
+        settle(values_all.at[chunk, pl.ds(0, peers - 1)], value_s)
+        settle(units_all.at[chunk, pl.ds(0, peers - 1)], unit_s)
+    best_out[...] = whole / nodes / jnp.sum(br_row, axis=1, keepdims=True)
 
 
 def evaluate(
@@ -421,6 +437,7 @@
     both = 2 * actions
     all_hands = ranks.shape[1]
     lanes = -(-boards_dev // 128) * 128
+    dma = pltpu.SemaphoreType.DMA
     return pl.pallas_call(
         functools.partial(kernel, leafs, hands, levels, actions),
         out_shape=(
@@ -436,8 +453,8 @@
             pltpu.VMEM((count, all_hands), jnp.int32),
             pltpu.VMEM((hands, count * both, width), BF16),
             pltpu.VMEM((hands, count * both, width), BF16),
-            pltpu.VMEM((hands, count, width), BF16),
-            pltpu.VMEM((hands, count, width), BF16),
+            pltpu.VMEM((hands, chunks, 8, width), BF16),
+            pltpu.VMEM((hands, chunks, 8, width), BF16),
             pltpu.VMEM((8, lanes), F32),
             pltpu.VMEM((leafs, 8, lanes), F32),
             pltpu.VMEM((hands, 1, width), F32),
@@ -448,18 +465,14 @@
             pltpu.VMEM((all_hands, all_hands), BF16),
             pltpu.VMEM((all_hands, all_hands), BF16),
             pltpu.VMEM((count, all_hands), F32),
-            pltpu.VMEM((chunks, hands, 8, width), F32),
-            pltpu.VMEM((chunks, hands, 8, width), F32),
-            pltpu.VMEM((chunks, leafs, hands, 8, width), F32),
-            pltpu.VMEM((hands, 8, 128), F32),
-            pltpu.VMEM((8, 128), F32),
-            pltpu.VMEM((leafs, 8, 128), F32),
-            sems(leafs), sems(leafs), sems(leafs), sems(leafs),
-            sems(chunks, hands), sems(chunks, hands), sems(hands), sems(hands), sems(hands), sems(hands),
-            sems(chunks, hands), sems(chunks, hands), sems(chunks, leafs), sems(chunks, leafs),
-            sems(hands), sems(hands), sems(leafs), sems(leafs),
-            pltpu.SemaphoreType.DMA((hands, chunks)),
-            pltpu.SemaphoreType.DMA((2,)),
+            pltpu.VMEM((chunks, hands, 8, width), jnp.int16),
+            pltpu.VMEM((chunks, leafs * hands, 8, width), jnp.int16),
+            pltpu.VMEM((chunks, 1, 128), F32),
+            pltpu.VMEM((chunks, leafs * hands, 1, 128), F32),
+            dma(()), dma((max(leafs // 2, 1),)), dma(()), dma(()), dma(()),
+            dma(()), dma((chunks,)), dma(()), dma(()), dma(()), dma(()),
+            dma(()), dma((chunks,)), dma(()), dma((chunks,)),
+            dma((chunks,)), dma((2,)),
         ],
         compiler_params=pltpu.CompilerParams(
             collective_id=0, has_side_effects=True, vmem_limit_bytes=VMEM_LIMIT

time: 55.3 us -> 41.8 us (0.76)
  Pallas kernels: 49.9 us -> 36.4 us
    pallas_call x1, Pallas kernels: 49.9 us -> 36.4 us  [evaluate(): pl.pallas_call(functools.partial(kernel, leafs, hands, levels, actions),...]
where the time goes in v2:
time: 41.8 us; the launch traced here: 41.6 us
  Pallas kernels  36.4 us (87%)
  local copies, waits for them, and re-layouts  2.8 us (7%)
  between operations  2.4 us (6%)
    pallas_call x1, Pallas kernels, evaluate(): pl.pallas_call(functools.partial(kernel, leafs, hands, levels, actions),...  36.4 us
    unnamed x2, local copies, waits for them, and re-layouts  2.8 us

profile of v2, /device:TPU:0, one launch (start us, length us, event | category | flops | bytes accessed | tf_op | source)
XLA Modules:
  0.0 41.6 jit_solution(3113139780244065844)
XLA Ops:
  0.6 36.4 %evaluate.1 = (f32[4,32,256]{2,1,0:T(8,128)}, f32[1,256]{1,0:T(1,128)}, f32[1,1]{1,0:T(1,128)}) custom-call(bf16[4,32,256]{2,1,0:T(8,128)(2,1)} %upper_ref.1, s32[3,256]{1,0:T(4,128)} %parent_ref.1, s32[1,96]{1,0:T(1,128)} %bitcast.22, s32[5,96]{1,0:T(8,128)} %bitcast.17, f32[1,256]{1,0:T(1,128)} %bitcast.19, f32[1,256]{1,0:T(1,128)} %bitcast.20, ...), custom_call_target="tpu_custom_call" | custom-call | tf_op jit(solution)/shard_map/evaluate/pallas_call | solution.py:441
  37.1 1.6 %copy.19 = f32[4,32,256]{2,1,0:T(8,128)} copy(f32[4,32,256]{2,1,0:T(8,128)} %get-tuple-element.12) | data formatting | bytes 262144
  38.6 1.2 %copy.20 = f32[256]{0:T(256)} copy(f32[256]{0:T(256)} %bitcast.21) | data formatting | bytes 2048

commit v3 on v2

--- a/solution.py
+++ b/solution.py
@@ -104,7 +104,7 @@
     leafs, hands, levels, actions,
     upper_ref, parent_ref, root_ref, board_ref, range_ref, br_ref, cards_ref, opp_ref, kind_ref, stake_ref,
     actions_ref, rank_ref, weight_ref,
-    level_out, root_out, best_out,
+    flat_out,
     every, weights, ranks_in, ratio, ratio_in, reach, reach_in, anc, anc_all, br_all,
     pad, board_columns, stake_lines, stake_rows, apart_ref, against_ref, scaled,
     ready, values_all, units, units_all,
@@ -328,6 +328,7 @@
                 rows = slice(part * width, (part + 1) * width)
                 order = rank_rows[i : i + 1, :] - rank_columns[rows, i : i + 1]
                 order = jnp.minimum(jnp.maximum(order, against_ref[rows, :]), apart_ref[rows, :])
+                order = order.astype(jnp.float8_e4m3fn)
                 shown = shown + jnp.dot(lines[part][i], order, preferred_element_type=F32)
             per_node = shown[0:actions] + folded[i * both + actions : (i + 1) * both]
             allowed = action_ids < actions_ref[first + i]
@@ -417,13 +418,21 @@
         for source in range(leafs):
             sums, share = add_leaf(chunk, source, sums)
             whole = whole + share
-    root_out[...] = sums[lines_dev : lines_dev + 1] / nodes
-    for k in range(levels):
-        level_out[k] = sums[k * nodes_dev : (k + 1) * nodes_dev]
+    flat_out[0:lines_dev] = sums[0:lines_dev]
     for chunk in range(chunks):
         settle(values_all.at[chunk, pl.ds(0, peers - 1)], value_s)
         settle(units_all.at[chunk, pl.ds(0, peers - 1)], unit_s)
-    best_out[...] = whole / nodes / jnp.sum(br_row, axis=1, keepdims=True)
+    best = whole / nodes / jnp.sum(br_row, axis=1, keepdims=True)
+    line = lax.broadcasted_iota(jnp.int32, (8, width), 0)
+    flat_out[lines_dev:] = jnp.where(line == 0, sums[lines_dev:] / nodes, best)
+
+
+def spread_kernel(flat_ref, level_out, root_out, best_out):
+    levels, nodes_dev, _ = level_out.shape
+    for k in range(levels):
+        level_out[k] = flat_ref[k * nodes_dev : (k + 1) * nodes_dev]
+    root_out[...] = flat_ref[levels * nodes_dev]
+    best_out[0, 0] = flat_ref[levels * nodes_dev + 1, 0]
 
 
 def evaluate(
@@ -438,15 +447,11 @@
     all_hands = ranks.shape[1]
     lanes = -(-boards_dev // 128) * 128
     dma = pltpu.SemaphoreType.DMA
-    return pl.pallas_call(
+    flat = pl.pallas_call(
         functools.partial(kernel, leafs, hands, levels, actions),
-        out_shape=(
-            jax.ShapeDtypeStruct((levels, nodes_dev, width), F32),
-            jax.ShapeDtypeStruct((1, width), F32),
-            jax.ShapeDtypeStruct((1, 1), F32),
-        ),
+        out_shape=jax.ShapeDtypeStruct((levels * nodes_dev + 8, width), F32),
         in_specs=[vmem()] * 10 + [pl.BlockSpec(memory_space=pltpu.SMEM), hbm(), hbm()],
-        out_specs=(vmem(), vmem(), vmem()),
+        out_specs=vmem(),
         scratch_shapes=[
             pltpu.VMEM((leafs, levels, nodes_dev, width), BF16),
             pltpu.VMEM((hands, count, span, width), BF16),
@@ -482,6 +487,17 @@
         upper, parents, roots, boards, opp_range, br_range, cards, opp_actions, kinds, stakes,
         br_actions, ranks, weights,
     )
+    return pl.pallas_call(
+        spread_kernel,
+        out_shape=(
+            jax.ShapeDtypeStruct((levels, nodes_dev, width), F32),
+            jax.ShapeDtypeStruct((width,), F32),
+            jax.ShapeDtypeStruct((1, 1), F32),
+        ),
+        in_specs=[vmem()],
+        out_specs=(vmem(), vmem(), pl.BlockSpec(memory_space=pltpu.SMEM)),
+        name="spread",
+    )(flat)
 
 
 def local(
@@ -524,7 +540,7 @@
         hands,
         actions,
     )
-    return (level_values, root[0], best[0, 0])
+    return (level_values, root, best[0, 0])
 
 
 def solution(mesh):

time: 41.8 us -> 38.3 us (0.916)
  local copies, waits for them, and re-layouts: 2.8 us -> 0 us
  between operations: 2.4 us -> 0.64 us
  Pallas kernels: 36.4 us -> 37.5 us
    unnamed x2 -> x0, local copies, waits for them, and re-layouts: 2.8 us -> none
    pallas_call x0 -> x1, Pallas kernels: none -> 1.58 us  [evaluate(): pl.pallas_call(spread_kernel, out_shape=(jax.ShapeDtypeStruct((levels, no...]
    pallas_call x1, Pallas kernels: 36.4 us -> 35.9 us  [evaluate(): pl.pallas_call(functools.partial(kernel, leafs, hands, levels, actions),...]
where the time goes in v3:
time: 38.3 us; the launch traced here: 38.1 us
  Pallas kernels  37.5 us (98%)
  between operations  0.64 us (2%)
    pallas_call x1, Pallas kernels, evaluate(): pl.pallas_call(functools.partial(kernel, leafs, hands, levels, actions),...  35.9 us
    pallas_call x1, Pallas kernels, evaluate(): pl.pallas_call(spread_kernel, out_shape=(jax.ShapeDtypeStruct((levels, no...  1.58 us

profile of v3, /device:TPU:0, one launch (start us, length us, event | category | flops | bytes accessed | tf_op | source)
XLA Modules:
  0.0 38.1 jit_solution(1034447470272564420)
XLA Ops:
  0.6 35.9 %evaluate.1.flat_ref = f32[136,256]{1,0:T(8,128)} custom-call(bf16[4,32,256]{2,1,0:T(8,128)(2,1)} %upper_ref.1, s32[3,256]{1,0:T(4,128)} %parent_ref.1, s32[1,96]{1,0:T(1,128)} %bitcast.20, s32[5,96]{1,0:T(8,128)} %bitcast.16, f32[1,256]{1,0:T(1,128)} %bitcast.18, f32[1,256]{1,0:T(1,128)} %bitcast.19, f32[8,1024]{1,0:T(8,128)} %constant.2.clone.cards_ref, ...), custom_call_target="tpu_custom_call" | custom-call | tf_op jit(solution)/shard_map/evaluate/pallas_call | solution.py:450
  36.5 1.6 %spread.1 = (f32[4,32,256]{2,1,0:T(8,128)}, f32[256]{0:T(256)}, f32[1,1]{1,0:T(1,128)}) custom-call(f32[136,256]{1,0:T(8,128)} %evaluate.1.flat_ref), custom_call_target="tpu_custom_call" | custom-call | tf_op jit(solution)/shard_map/spread/pallas_call | solution.py:490

commit v4 on v3

--- a/solution.py
+++ b/solution.py
@@ -12,6 +12,7 @@
 VMEM_LIMIT = 60 * 1024 * 1024
 F32 = jnp.float32
 BF16 = jnp.bfloat16
+F8 = jnp.float8_e4m3fn
 
 
 def hand_cards(number):
@@ -106,7 +107,7 @@
     actions_ref, rank_ref, weight_ref,
     flat_out,
     every, weights, ranks_in, ratio, ratio_in, reach, reach_in, anc, anc_all, br_all,
-    pad, board_columns, stake_lines, stake_rows, apart_ref, against_ref, scaled,
+    pad, board_columns, stake_lines, stake_rows, apart_ref, against_ref, apart_small, order_ref, scaled,
     ready, values_all, units, units_all,
     up_s, up_r, pass_r, anc_s, anc_r, ratio_s, ratio_r, reach_s, reach_r, br_s, br_r,
     value_s, value_r, unit_s, unit_r, load_sem, own_sem,
@@ -244,17 +245,64 @@
     low = cards_ref[0:1, :]
     high = cards_ref[1:2, :]
     card_columns = cards_ref[...].T
+    deck_lanes = lax.broadcasted_iota(jnp.int32, (width, 128), 1).astype(F32)
+    deck_rows = lax.broadcasted_iota(jnp.int32, (128, all_hands), 0).astype(F32)
+    holds = jnp.where((deck_rows == low) | (deck_rows == high), 1.0, 0.0).astype(BF16)
     for part in range(hands):
-        if part == hands // 2:
-            pass_on([dist for dist in steps if dist in (1, ring - 1)])
         rows = slice(part * width, (part + 1) * width)
-        low_col = card_columns[rows, 0:1]
-        high_col = card_columns[rows, 1:2]
-        hit = (low_col == low) | (low_col == high) | (high_col == low) | (high_col == high)
-        apart_ref[rows, :] = jnp.where(hit, 0.0, 1.0).astype(BF16)
-        against_ref[rows, :] = jnp.where(hit, 0.0, -1.0).astype(BF16)
-
-    pass_on([dist for dist in steps if dist not in (1, ring - 1)])
+        held = (deck_lanes == card_columns[rows, 0:1]) | (deck_lanes == card_columns[rows, 1:2])
+        held = jnp.where(held, 1.0, 0.0).astype(BF16)
+        common = jnp.dot(held, holds, preferred_element_type=F32).astype(BF16)
+        apart = jnp.maximum(1.0 - common, 0.0)
+        apart_ref[rows, :] = apart
+        against_ref[rows, :] = jnp.minimum(common - 1.0, 0.0)
+        apart_small[rows, :] = apart.astype(F8)
+
+    own_ranks.wait()
+    ranks = ((ranks_in[...] % 128) + 128).astype(F32)
+    octave = ranks_in[...] // 128
+    for bit in (1, 2, 4, 8, 16, 32):
+        ranks = ranks * jnp.where(octave // bit % 2 == 1, float(2**bit), 1.0)
+    scaled[...] = ranks
+
+    def compare(chunk, strips):
+        rank_rows = scaled[pl.ds(pl.multiple_of(chunk * 8, 8), 8), :]
+        rank_columns = rank_rows.T.astype(BF16)
+        rank_rows = rank_rows.astype(BF16)
+        for first in strips:
+            lanes_of = slice(first, first + width)
+            across = [jnp.broadcast_to(rank_rows[i : i + 1, lanes_of], (32, width)) for i in range(8)]
+            for top in range(0, all_hands, 32):
+                rows = slice(top, top + 32)
+                against = against_ref[rows, lanes_of]
+                apart = apart_ref[rows, lanes_of]
+                for i in range(8):
+                    sign = across[i] - rank_columns[rows, i : i + 1]
+                    sign = jnp.minimum(jnp.maximum(sign, against), apart)
+                    order_ref[chunk * 8 + i, rows, lanes_of] = sign.astype(F8)
+
+    outer = [dist for dist in steps if dist in (1, ring - 1)]
+    inner = [dist for dist in steps if dist not in (1, ring - 1)]
+    parity = lax.rem(hand, 2)
+
+    def pass_if(which, dists):
+        @pl.when(parity == which)
+        def _():
+            pass_on(dists)
+
+    strips = list(range(0, all_hands, width))
+    half = len(strips) // 2
+    pass_if(1, outer)
+    compare(0, strips[:half])
+    pass_if(1, inner)
+    compare(0, strips[half:])
+    pass_if(0, outer)
+    early = min(chunks, 2)
+    for chunk in range(1, early):
+        compare(chunk, strips[:half])
+    pass_if(0, inner)
+    for chunk in range(1, early):
+        compare(chunk, strips[half:])
     for chunk in range(chunks):
         fold(hand, chunk, ratio_in)
 
@@ -266,13 +314,6 @@
         column = board_columns[0:boards, card : card + 1]
         free = jnp.where((column == own_low) | (column == own_high), 0.0, free)
     free = free * cards_ref[3:4, own_lanes]
-
-    own_ranks.wait()
-    ranks = ((ranks_in[...] % 128) + 128).astype(F32)
-    octave = ranks_in[...] // 128
-    for bit in (1, 2, 4, 8, 16, 32):
-        ranks = ranks * jnp.where(octave // bit % 2 == 1, float(2**bit), 1.0)
-    scaled[...] = ranks
 
     own_upper.wait()
     up_direct[0].wait_recv()
@@ -294,45 +335,43 @@
     action_ids = lax.broadcasted_iota(jnp.int32, (actions, 1), 0)
     settle(br_all.at[pl.ds(0, hands - 1)], br_r)
     br_row = jnp.concatenate([br_all[part] for part in range(hands)], axis=1)
-    settle(reach.at[pl.ds(0, hands - 1)], reach_r)
-
-    def values(chunk):
+
+    def partial(chunk, group):
+        lines = []
+        folded = jnp.zeros((8 * both, all_hands), F32)
+        for part in group:
+            rows = slice(part * width, (part + 1) * width)
+            pieces = []
+            reach_rows = reach_in[part, chunk].astype(F32)
+            for i in range(8):
+                b = chunk * 8 + i
+                row = ratio_in[part, pl.ds(pl.multiple_of(b * both, both), both), :].astype(F32)
+                pieces.append((row * reach_rows[i : i + 1, :]).astype(BF16))
+            lines.append((rows, pieces))
+            folded = folded + jnp.dot(
+                jnp.concatenate(pieces, axis=0), apart_small[rows, :], preferred_element_type=F32
+            )
+        nodes_of = []
+        for i in range(8):
+            shown = jnp.zeros((both, all_hands), F32)
+            for rows, pieces in lines:
+                shown = shown + jnp.dot(
+                    pieces[i], order_ref[chunk * 8 + i, rows, :], preferred_element_type=F32
+                )
+            nodes_of.append(shown[0:actions] + folded[i * both + actions : (i + 1) * both])
+        return nodes_of
+
+    def finish(chunk, nodes_of):
         first = pl.multiple_of(hand * count + chunk * 8, 8)
         cards_on = board_columns[pl.ds(first, 8), :]
         open_hands = jnp.ones((8, all_hands), F32)
         for card in range(5):
             column = cards_on[:, card : card + 1]
             open_hands = jnp.where((column == low) | (column == high), 0.0, open_hands)
-        rank_rows = scaled[pl.ds(pl.multiple_of(chunk * 8, 8), 8), :]
-        rank_columns = rank_rows.T.astype(BF16)
-        rank_rows = rank_rows.astype(BF16)
-        lines = []
-        folded = jnp.zeros((8 * both, all_hands), F32)
-        for part in range(hands):
-            pieces = []
-            reach_rows = reach_in[part, chunk].astype(F32)
-            for i in range(8):
-                b = chunk * 8 + i
-                row = ratio_in[part, pl.ds(pl.multiple_of(b * both, both), both), :].astype(F32)
-                pieces.append((row * reach_rows[i : i + 1, :]).astype(BF16))
-            lines.append(pieces)
-            folded = folded + jnp.dot(
-                jnp.concatenate(pieces, axis=0),
-                apart_ref[part * width : (part + 1) * width, :],
-                preferred_element_type=F32,
-            )
         best_rows = []
         for i in range(8):
-            shown = jnp.zeros((both, all_hands), F32)
-            for part in range(hands):
-                rows = slice(part * width, (part + 1) * width)
-                order = rank_rows[i : i + 1, :] - rank_columns[rows, i : i + 1]
-                order = jnp.minimum(jnp.maximum(order, against_ref[rows, :]), apart_ref[rows, :])
-                order = order.astype(jnp.float8_e4m3fn)
-                shown = shown + jnp.dot(lines[part][i], order, preferred_element_type=F32)
-            per_node = shown[0:actions] + folded[i * both + actions : (i + 1) * both]
             allowed = action_ids < actions_ref[first + i]
-            best_rows.append(jnp.max(jnp.where(allowed, per_node, -1e30), axis=0, keepdims=True))
+            best_rows.append(jnp.max(jnp.where(allowed, nodes_of[i], -1e30), axis=0, keepdims=True))
         best = jnp.concatenate(best_rows, axis=0) * (open_hands * PAYOFF_UNIT)
         peak = jnp.max(jnp.abs(best), axis=1, keepdims=True) * (1.0 / 32640.0)
         unit = jnp.full((8, 1), 2.0**16, F32)
@@ -352,40 +391,65 @@
 
     peers = leafs * hands
 
-    def send_values(chunk, k):
-        to_hand = lax.rem(hand + k % hands, hands)
-        target = {"leaf": lax.rem(leaf + k // hands, leafs), "hand": to_hand}
-        pltpu.make_async_remote_copy(
-            src_ref=ready.at[chunk, to_hand],
-            dst_ref=values_all.at[chunk, leaf * hands + hand],
-            send_sem=value_s,
-            recv_sem=value_r.at[chunk],
-            device_id=target,
-            device_id_type=pl.DeviceIdType.MESH,
-        ).start()
-        pltpu.make_async_remote_copy(
-            src_ref=units.at[chunk],
-            dst_ref=units_all.at[chunk, leaf * hands + hand],
-            send_sem=unit_s,
-            recv_sem=unit_r.at[chunk],
-            device_id=target,
-            device_id_type=pl.DeviceIdType.MESH,
-        ).start()
+    behind = len(inner) * hands
+
+    def ship(chunk, what, slots, target, sem_set):
+        for kind, source, place in what:
+            pltpu.make_async_remote_copy(
+                src_ref=source,
+                dst_ref=place.at[chunk, slots],
+                send_sem=(value_s, unit_s)[kind],
+                recv_sem=(value_r, unit_r)[kind].at[sem_set, chunk],
+                device_id=target,
+                device_id_type=pl.DeviceIdType.MESH,
+            ).start()
+
+    def send_chunk(chunk, direct):
+        own = leaf * hands + hand
+        for dist in range(ring):
+            for cross in (0, 1):
+                if cross and dist in inner and not direct:
+                    continue
+                to_leaf = around(dist)
+                if cross:
+                    to_leaf = to_leaf + 1 - 2 * side
+                group = 1 if dist in inner and not direct else 0
+                for dh in range(hands):
+                    if dist == 0 and not cross and dh == 0:
+                        continue
+                    to_hand = lax.rem(hand + dh, hands)
+                    what = [(0, ready.at[chunk, to_hand], values_all), (1, units.at[chunk], units_all)]
+                    ship(chunk, what, own, {"leaf": to_leaf, "hand": to_hand}, group)
+        values_all[chunk, own] = ready[chunk, hand]
+        units_all[chunk, own] = units[chunk]
+
+    def collect(chunk, blocks, sem_set):
+        if blocks:
+            settle(values_all.at[chunk, pl.ds(0, blocks)], value_r.at[sem_set, chunk])
+            settle(units_all.at[chunk, pl.ds(0, blocks)], unit_r.at[sem_set, chunk])
+
+    def relay_chunk(chunk):
+        collect(chunk, behind, 1)
+        for dist in inner:
+            slots = pl.ds(around(dist) * hands, hands)
+            what = [(0, values_all.at[chunk, slots], values_all), (1, units_all.at[chunk, slots], units_all)]
+            ship(chunk, what, slots, {"leaf": twin}, 2)
 
     def one_chunk(chunk, carry):
+        finish(chunk, partial(chunk, list(range(hands))))
+        send_chunk(chunk, False)
+        return carry
+
+    for chunk in range(early, chunks):
+        compare(chunk, strips)
+    for chunk in range(chunks):
         settle(ratio.at[pl.ds(0, hands - 1), pl.ds(0, 8 * both)], ratio_r.at[chunk])
-        values(chunk)
-
-        def one(k, carry):
-            send_values(chunk, k)
-            return carry
-
-        lax.fori_loop(1, peers, one, 0, unroll=peers <= 32)
-        values_all[chunk, leaf * hands + hand] = ready[chunk, hand]
-        units_all[chunk, leaf * hands + hand] = units[chunk]
-        return carry
-
-    lax.fori_loop(0, chunks, one_chunk, 0)
+    settle(reach.at[pl.ds(0, hands - 1)], reach_r)
+    lax.fori_loop(0, chunks - 1, one_chunk, 0)
+    finish(chunks - 1, partial(chunks - 1, list(range(hands))))
+    send_chunk(chunks - 1, True)
+    for chunk in range(chunks - 1):
+        relay_chunk(chunk)
     settle(ratio.at[pl.ds(0, hands - 1)], ratio_s)
     settle(reach.at[pl.ds(0, hands - 1)], reach_s)
     settle(br_all.at[pl.ds(0, hands - 1)], br_s)
@@ -394,29 +458,39 @@
     settle(anc_all.at[pl.ds(0, leafs - 1)], anc_s)
     lines_dev = levels * nodes_dev
     block = hands * 8
-    node_rows = leaf * nodes_dev + lax.broadcasted_iota(jnp.int32, (nodes_dev, block), 0)
-    node_rows = node_rows.astype(F32)
-
-    def add_leaf(chunk, source, sums):
-        own = pl.ds(source * hands, hands)
-        part = values_all[chunk, own].astype(jnp.int32).astype(F32).reshape(block, width)
+    together = max(width // block, 1)
+    groups = [list(range(k, min(k + together, leafs))) for k in range(0, leafs, together)]
+
+    def add_group(chunk, group, sums):
+        own = pl.ds(group[0] * hands, len(group) * hands)
+        tall = len(group) * block
+        lines = [anc_all[source][:, chunk * block : (chunk + 1) * block] for source in group]
+        lines = jnp.concatenate(lines, axis=1)
+        node_rows = leaf * nodes_dev + lax.broadcasted_iota(jnp.int32, (nodes_dev, tall), 0)
+        node_rows = node_rows.astype(F32)
+        rows = [
+            jnp.sum(units_all[chunk, source * hands : (source + 1) * hands], axis=0) for source in group
+        ]
+        unit = jnp.concatenate([row[:, 0:block] for row in rows], axis=1)
+        part = values_all[chunk, own].astype(jnp.int32).astype(F32).reshape(tall, width)
         coarse = part.astype(BF16)
         fine = (part - coarse.astype(F32)).astype(BF16)
-        lines = anc_all[source][:, chunk * block : (chunk + 1) * block]
-        row = jnp.sum(units_all[chunk, own], axis=0)
-        unit = row[:, 0:block]
         pick = [jnp.where(lines[k : k + 1, :] == node_rows, unit, 0.0) for k in range(levels)]
-        pick = jnp.concatenate(pick + [jnp.broadcast_to(unit, (8, block))], axis=0).astype(BF16)
+        pick = jnp.concatenate(pick + [jnp.broadcast_to(unit, (8, tall))], axis=0).astype(BF16)
         sums = sums + jnp.dot(pick, coarse, preferred_element_type=F32)
-        return sums + jnp.dot(pick, fine, preferred_element_type=F32), row[:, block : block + 1]
+        share = sum(row[:, block : block + 1] for row in rows)
+        return sums + jnp.dot(pick, fine, preferred_element_type=F32), share
 
     sums = jnp.zeros((lines_dev + 8, width), F32)
     whole = jnp.zeros((1, 1), F32)
     for chunk in range(chunks):
-        settle(values_all.at[chunk, pl.ds(0, peers - 1)], value_r.at[chunk])
-        settle(units_all.at[chunk, pl.ds(0, peers - 1)], unit_r.at[chunk])
-        for source in range(leafs):
-            sums, share = add_leaf(chunk, source, sums)
+        if chunk < chunks - 1:
+            collect(chunk, peers - 1 - 2 * behind, 0)
+            collect(chunk, behind, 2)
+        else:
+            collect(chunk, peers - 1, 0)
+        for group in groups:
+            sums, share = add_group(chunk, group, sums)
             whole = whole + share
     flat_out[0:lines_dev] = sums[0:lines_dev]
     for chunk in range(chunks):
@@ -469,6 +543,8 @@
             pltpu.VMEM((lanes, span), F32),
             pltpu.VMEM((all_hands, all_hands), BF16),
             pltpu.VMEM((all_hands, all_hands), BF16),
+            pltpu.VMEM((all_hands, all_hands), F8),
+            pltpu.VMEM((count, all_hands, all_hands), F8),
             pltpu.VMEM((count, all_hands), F32),
             pltpu.VMEM((chunks, hands, 8, width), jnp.int16),
             pltpu.VMEM((chunks, leafs * hands, 8, width), jnp.int16),
@@ -476,7 +552,7 @@
             pltpu.VMEM((chunks, leafs * hands, 1, 128), F32),
             dma(()), dma((max(leafs // 2, 1),)), dma(()), dma(()), dma(()),
             dma(()), dma((chunks,)), dma(()), dma(()), dma(()), dma(()),
-            dma(()), dma((chunks,)), dma(()), dma((chunks,)),
+            dma(()), dma((3, chunks)), dma(()), dma((3, chunks)),
             dma((chunks,)), dma((2,)),
         ],
         compiler_params=pltpu.CompilerParams(

time: 38.3 us -> 37.2 us (0.971)
  Pallas kernels: 37.5 us -> 36.2 us
    pallas_call x1, Pallas kernels: 35.9 us -> 34.6 us  [evaluate(): pl.pallas_call(functools.partial(kernel, leafs, hands, levels, actions),...]
where the time goes in v4:
time: 37.2 us; the launch traced here: 37 us
  Pallas kernels  36.2 us (97%)
  between operations  0.8 us (2%)
    pallas_call x1, Pallas kernels, evaluate(): pl.pallas_call(functools.partial(kernel, leafs, hands, levels, actions),...  34.6 us
    pallas_call x1, Pallas kernels, evaluate(): pl.pallas_call(spread_kernel, out_shape=(jax.ShapeDtypeStruct((levels, no...  1.58 us

profile of v4, /device:TPU:0, one launch (start us, length us, event | category | flops | bytes accessed | tf_op | source)
XLA Modules:
  0.0 37.0 jit_solution(10628621426146083073)
XLA Ops:
  0.6 34.6 %evaluate.1.flat_ref = f32[136,256]{1,0:T(8,128)} custom-call(bf16[4,32,256]{2,1,0:T(8,128)(2,1)} %upper_ref.1, s32[3,256]{1,0:T(4,128)} %parent_ref.1, s32[1,96]{1,0:T(1,128)} %bitcast.20, s32[5,96]{1,0:T(8,128)} %bitcast.16, f32[1,256]{1,0:T(1,128)} %bitcast.18, f32[1,256]{1,0:T(1,128)} %bitcast.19, f32[8,1024]{1,0:T(8,128)} %constant.2.clone.cards_ref, ...), custom_call_target="tpu_custom_call" | custom-call | tf_op jit(solution)/shard_map/evaluate/pallas_call | solution.py:524
  35.2 1.6 %spread.1 = (f32[4,32,256]{2,1,0:T(8,128)}, f32[256]{0:T(256)}, f32[1,1]{1,0:T(1,128)}) custom-call(f32[136,256]{1,0:T(8,128)} %evaluate.1.flat_ref), custom_call_target="tpu_custom_call" | custom-call | tf_op jit(solution)/shard_map/spread/pallas_call | solution.py:566

commit v5 on v4

--- a/solution.py
+++ b/solution.py
@@ -406,8 +406,8 @@
 
     def send_chunk(chunk, direct):
         own = leaf * hands + hand
-        for dist in range(ring):
-            for cross in (0, 1):
+        for dist in inner + outer + [0]:
+            for cross in (1, 0):
                 if cross and dist in inner and not direct:
                     continue
                 to_leaf = around(dist)

time: 37.2 us -> 36.8 us (0.989)
  Pallas kernels: 36.2 us -> 35.8 us
where the time goes in v5:
time: 36.8 us; the launch traced here: 36.6 us
  Pallas kernels  35.8 us (97%)
  between operations  0.8 us (2%)
    pallas_call x1, Pallas kernels, evaluate(): pl.pallas_call(functools.partial(kernel, leafs, hands, levels, actions),...  34.2 us
    pallas_call x1, Pallas kernels, evaluate(): pl.pallas_call(spread_kernel, out_shape=(jax.ShapeDtypeStruct((levels, no...  1.58 us

profile of v5, /device:TPU:0, one launch (start us, length us, event | category | flops | bytes accessed | tf_op | source)
XLA Modules:
  0.0 36.6 jit_solution(2995171068090972923)
XLA Ops:
  0.6 34.2 %evaluate.1.flat_ref = f32[136,256]{1,0:T(8,128)} custom-call(bf16[4,32,256]{2,1,0:T(8,128)(2,1)} %upper_ref.1, s32[3,256]{1,0:T(4,128)} %parent_ref.1, s32[1,96]{1,0:T(1,128)} %bitcast.20, s32[5,96]{1,0:T(8,128)} %bitcast.16, f32[1,256]{1,0:T(1,128)} %bitcast.18, f32[1,256]{1,0:T(1,128)} %bitcast.19, f32[8,1024]{1,0:T(8,128)} %constant.2.clone.cards_ref, ...), custom_call_target="tpu_custom_call" | custom-call | tf_op jit(solution)/shard_map/evaluate/pallas_call | solution.py:524
  34.9 1.6 %spread.1 = (f32[4,32,256]{2,1,0:T(8,128)}, f32[256]{0:T(256)}, f32[1,1]{1,0:T(1,128)}) custom-call(f32[136,256]{1,0:T(8,128)} %evaluate.1.flat_ref), custom_call_target="tpu_custom_call" | custom-call | tf_op jit(solution)/shard_map/spread/pallas_call | solution.py:566
